TPU v7x, 512 devices: a whole 4x4x16 slice. The times are simulated.
512 devices in a mesh: tok: 64 (over x, z), blk: 8 (over y, core).
Axes of the slice: x: 4, y: 4, z: 16, core: 2. Of those that a mesh axis runs over, the one named last changes fastest.
Arguments:
- activations: bfloat16 [16384, 2048], P('tok', 'blk'), may hold values from -16 to 16
Outputs:
- factored: float32 [2048, 2048], P('blk', 'tok')
All inputs are finite; a program needn't handle non-finite values.
Results may differ from a plain program's by a relative error of at most 0.0003.
Values may be sent and summed in bfloat16 or wider, within the bound.
A program may use at most 64 MiB of HBM per device.

v0:
```python
import jax
import jax.numpy as jnp
from jax import lax
from jax.sharding import Mesh
from jax.sharding import PartitionSpec as P

STEPS = 4
TOK = ("tok_0", "tok_1")
BLK = ("blk_0", "blk_1")
TOK_BLK = ("tok_0", "tok_1", "blk_0", "blk_1")


def joined_along(tiles, dim):
    tiles = jnp.moveaxis(tiles, 0, dim)
    shape = tiles.shape
    return tiles.reshape(*shape[:dim], shape[dim] * shape[dim + 1], *shape[dim + 2 :])


def from_everyone(x, axis):
    length = lax.axis_size(axis)
    return lax.all_to_all(jnp.broadcast_to(x[None], (length, *x.shape)), axis, 0, 0, tiled=True)


def gathered_copies(x, axis, dim):
    return joined_along(from_everyone(x, axis), dim)


def over_axes(x, axes):
    for axis in axes:
        x = lax.psum(x, axis)
    return x


def spread(x, axes, root):
    x = jnp.where(lax.axis_index(axes) == root, x, jnp.zeros_like(x))
    for axis in axes:
        x = lax.psum(x, axis)
    return x


def shards(activations):
    rows_block = activations.shape[1]
    tok_count = lax.axis_size(TOK)
    blk_count = lax.axis_size(BLK)
    full_width = rows_block * blk_count
    strip_width = full_width // tok_count
    total_tokens = activations.shape[0] * tok_count
    partial_rows = lax.dot_general(
        activations,
        gathered_copies(activations, BLK, 1),
        (((0,), (0,)), ((), ())),
        preferred_element_type=jnp.float32,
    )
    pieces = lax.all_to_all(partial_rows, TOK, split_axis=1, concat_axis=0, tiled=True)
    hessian_tile = jnp.sum(pieces.reshape(tok_count, rows_block, strip_width), axis=0) * (
        2.0 / total_tokens
    )
    tok_index = lax.axis_index(TOK)
    blk_index = lax.axis_index(BLK)
    row_ids = blk_index * rows_block + jnp.arange(rows_block, dtype=jnp.int32)[:, None]
    col_ids = tok_index * strip_width + jnp.arange(strip_width, dtype=jnp.int32)[None, :]
    on_diag = row_ids == col_ids
    trace_total = over_axes(jnp.sum(jnp.where(on_diag, hessian_tile, 0.0)), TOK_BLK)
    hessian_tile = hessian_tile + jnp.where(on_diag, 0.01 * trace_total / full_width, 0.0)
    positions = jnp.arange(full_width, dtype=jnp.int32)[:, None]
    for section in range(STEPS):
        strip_rows = spread(hessian_tile, TOK, section)
        column = gathered_copies(strip_rows, BLK, 0)
        pivot_block = column[section * strip_width : (section + 1) * strip_width]
        factor = jnp.linalg.cholesky(pivot_block)
        solved = jax.scipy.linalg.solve_triangular(factor, column.T, lower=True).T
        solved = jnp.where(positions >= section * strip_width, solved, 0.0)
        own_rows = lax.dynamic_slice_in_dim(solved, blk_index * rows_block, rows_block, 0)
        own_cols = lax.dynamic_slice_in_dim(solved, tok_index * strip_width, strip_width, 0)
        update = jnp.dot(own_rows, own_cols.T, precision=lax.Precision.HIGHEST)
        hessian_tile = jnp.where(
            tok_index > section,
            hessian_tile - update,
            jnp.where(tok_index == section, own_rows, hessian_tile),
        )
    return jnp.where(row_ids >= col_ids, hessian_tile, 0.0)


def solution(mesh):
    finer = Mesh(mesh.devices.reshape(4, 16, 4, 2), ("tok_0", "tok_1", "blk_0", "blk_1"))
    placed = (P(TOK, BLK),)
    return jax.shard_map(
        shards, mesh=finer, in_specs=placed, out_specs=P(BLK, TOK), check_vma=False
    )
```

profile of v0, /device:TPU:1, one launch (start us, length us, event | category | flops | bytes accessed | tf_op | source)
XLA Modules:
  0.0 545.0 jit_solution(8024689123034362587)
XLA Ops:
  1.2 24.2 %all_to_all.35 = bf16[8,256,256]{1,2,0:T(8,128)(2,1)S(1)} all-to-all(bf16[8,256,256]{1,2,0:T(8,128)(2,1)S(1)} %broadcast_in_dim.73), channel_id=1, replica_groups=mesh['tok_0'=4,'tok_1'=16,'blk_0'=4,'blk_1'=2] {'blk_0','blk_1'}, dimensions={0} | all-to-all | bytes 2097152 | tf_op jit(solution)/shard_map/all_to_all | solution.py:21
  27.1 14.8 %all-to-all-start.1 = ((f32[256,64,32]{0,2,1:T(8,128)}), f32[256,64,32]{0,2,1:T(8,128)S(1)}, u32[]{:S(2)}, u32[]{:S(2)}) async-start(f32[256,64,32]{0,2,1:T(8,128)} %fusion.10), calls=%async_computation.1 | async-start | bytes 4194304 | tf_op jit(solution)/shard_map/all_to_all | solution.py:54
  42.0 91.9 %all-to-all-done.1 = f32[256,64,32]{0,2,1:T(8,128)S(1)} async-done(((f32[256,64,32]{0,2,1:T(8,128)}), f32[256,64,32]{0,2,1:T(8,128)S(1)}, u32[]{:S(2)}, u32[]{:S(2)}) %all-to-all-start.1) | async-done | bytes 2097184 | tf_op jit(solution)/shard_map/all_to_all | solution.py:54
  134.7 8.2 %psum.84 = f32[]{:T(128)} all-reduce(f32[]{:T(128)} %fusion.12), channel_id=1, replica_groups=mesh['tok_0'=4,'tok_1'=16,'blk_0'=4,'blk_1'=2] {'tok_0'}, use_global_device_ids=true, to_apply=%region_2.3 | all-reduce | flops 1 | bytes 8 | tf_op jit(solution)/shard_map/psum | solution.py:30
  142.9 27.8 %psum.85 = f32[]{:T(128)} all-reduce(f32[]{:T(128)} %psum.84), channel_id=1, replica_groups=mesh['tok_0'=4,'tok_1'=16,'blk_0'=4,'blk_1'=2] {'tok_1'}, use_global_device_ids=true, to_apply=%region_3.4 | all-reduce | flops 1 | bytes 8 | tf_op jit(solution)/shard_map/psum | solution.py:30
  170.7 7.5 %psum.86 = f32[]{:T(128)} all-reduce(f32[]{:T(128)} %psum.85), channel_id=1, replica_groups=mesh['tok_0'=4,'tok_1'=16,'blk_0'=4,'blk_1'=2] {'blk_0'}, use_global_device_ids=true, to_apply=%region_4.5 | all-reduce | flops 1 | bytes 8 | tf_op jit(solution)/shard_map/psum | solution.py:30
  178.2 16.2 %psum.87 = f32[]{:T(128)} all-reduce(f32[]{:T(128)} %psum.86), channel_id=1, replica_groups=mesh['tok_0'=4,'tok_1'=16,'blk_0'=4,'blk_1'=2] {'blk_1'}, use_global_device_ids=true, to_apply=%region_5.6 | all-reduce | flops 1 | bytes 8 | tf_op jit(solution)/shard_map/psum | solution.py:30
  195.1 10.9 %psum.88 = f32[256,32]{0,1:T(8,128)S(1)} all-reduce(f32[256,32]{0,1:T(8,128)S(1)} %fusion.18), channel_id=1, replica_groups=mesh['tok_0'=4,'tok_1'=16,'blk_0'=4,'blk_1'=2] {'tok_0'}, use_global_device_ids=true, to_apply=%region_6.7 | all-reduce | flops 8192 | bytes 65536 | tf_op jit(solution)/shard_map/psum | solution.py:37
  206.1 39.5 %psum.89 = f32[256,32]{0,1:T(8,128)S(1)} all-reduce(f32[256,32]{0,1:T(8,128)S(1)} %psum.88), channel_id=1, replica_groups=mesh['tok_0'=4,'tok_1'=16,'blk_0'=4,'blk_1'=2] {'tok_1'}, use_global_device_ids=true, to_apply=%region_7.8 | all-reduce | flops 8192 | bytes 65536 | tf_op jit(solution)/shard_map/psum | solution.py:37
  246.3 20.8 %all-to-all-start.2 = ((f32[8,256,32]{1,2,0:T(8,128)}), f32[8,256,32]{1,2,0:T(8,128)S(1)}, u32[]{:S(2)}, u32[]{:S(2)}) async-start(f32[8,256,32]{1,2,0:T(8,128)} %broadcast_in_dim.76), calls=%async_computation.2 | async-start | bytes 524288 | tf_op jit(solution)/shard_map/all_to_all | solution.py:21
  267.1 6.5 %all-to-all-done.2 = f32[8,256,32]{1,2,0:T(8,128)S(1)} async-done(((f32[8,256,32]{1,2,0:T(8,128)}), f32[8,256,32]{1,2,0:T(8,128)S(1)}, u32[]{:S(2)}, u32[]{:S(2)}) %all-to-all-start.2) | async-done | bytes 262176 | tf_op jit(solution)/shard_map/all_to_all | solution.py:21
  281.2 12.4 %psum.90 = f32[256,32]{0,1:T(8,128)S(1)} all-reduce(f32[256,32]{0,1:T(8,128)S(1)} %get-tuple-element.6), channel_id=1, replica_groups=mesh['tok_0'=4,'tok_1'=16,'blk_0'=4,'blk_1'=2] {'tok_0'}, use_global_device_ids=true, to_apply=%region_10.13 | all-reduce | flops 8192 | bytes 65536 | tf_op jit(solution)/shard_map/psum | solution.py:37
  293.6 39.1 %psum.91 = f32[256,32]{0,1:T(8,128)S(1)} all-reduce(f32[256,32]{0,1:T(8,128)S(1)} %psum.90), channel_id=1, replica_groups=mesh['tok_0'=4,'tok_1'=16,'blk_0'=4,'blk_1'=2] {'tok_1'}, use_global_device_ids=true, to_apply=%region_11.14 | all-reduce | flops 8192 | bytes 65536 | tf_op jit(solution)/shard_map/psum | solution.py:37
  333.4 21.8 %all-to-all-start.3 = ((f32[8,256,32]{1,2,0:T(8,128)}), f32[8,256,32]{1,2,0:T(8,128)S(1)}, u32[]{:S(2)}, u32[]{:S(2)}) async-start(f32[8,256,32]{1,2,0:T(8,128)} %broadcast_in_dim.78), calls=%async_computation.3 | async-start | bytes 524288 | tf_op jit(solution)/shard_map/all_to_all | solution.py:21
  355.2 6.5 %all-to-all-done.3 = f32[8,256,32]{1,2,0:T(8,128)S(1)} async-done(((f32[8,256,32]{1,2,0:T(8,128)}), f32[8,256,32]{1,2,0:T(8,128)S(1)}, u32[]{:S(2)}, u32[]{:S(2)}) %all-to-all-start.3) | async-done | bytes 262176 | tf_op jit(solution)/shard_map/all_to_all | solution.py:21
  361.9 2.9 cholesky.85
  369.4 10.9 %psum.92 = f32[256,32]{0,1:T(8,128)S(1)} all-reduce(f32[256,32]{0,1:T(8,128)S(1)} %get-tuple-element.9), channel_id=1, replica_groups=mesh['tok_0'=4,'tok_1'=16,'blk_0'=4,'blk_1'=2] {'tok_0'}, use_global_device_ids=true, to_apply=%region_12.15 | all-reduce | flops 8192 | bytes 65536 | tf_op jit(solution)/shard_map/psum | solution.py:37
  380.3 39.3 %psum.93 = f32[256,32]{0,1:T(8,128)S(1)} all-reduce(f32[256,32]{0,1:T(8,128)S(1)} %psum.92), channel_id=1, replica_groups=mesh['tok_0'=4,'tok_1'=16,'blk_0'=4,'blk_1'=2] {'tok_1'}, use_global_device_ids=true, to_apply=%region_13.16 | all-reduce | flops 8192 | bytes 65536 | tf_op jit(solution)/shard_map/psum | solution.py:37
  420.4 21.7 %all-to-all-start.4 = ((f32[8,256,32]{1,2,0:T(8,128)}), f32[8,256,32]{1,2,0:T(8,128)S(1)}, u32[]{:S(2)}, u32[]{:S(2)}) async-start(f32[8,256,32]{1,2,0:T(8,128)} %broadcast_in_dim.81), calls=%async_computation.4 | async-start | bytes 524288 | tf_op jit(solution)/shard_map/all_to_all | solution.py:21
  442.1 6.5 %all-to-all-done.4 = f32[8,256,32]{1,2,0:T(8,128)S(1)} async-done(((f32[8,256,32]{1,2,0:T(8,128)}), f32[8,256,32]{1,2,0:T(8,128)S(1)}, u32[]{:S(2)}, u32[]{:S(2)}) %all-to-all-start.4) | async-done | bytes 262176 | tf_op jit(solution)/shard_map/all_to_all | solution.py:21
  456.3 12.4 %psum.94 = f32[256,32]{0,1:T(8,128)S(1)} all-reduce(f32[256,32]{0,1:T(8,128)S(1)} %get-tuple-element.11), channel_id=1, replica_groups=mesh['tok_0'=4,'tok_1'=16,'blk_0'=4,'blk_1'=2] {'tok_0'}, use_global_device_ids=true, to_apply=%region_14.17 | all-reduce | flops 8192 | bytes 65536 | tf_op jit(solution)/shard_map/psum | solution.py:37
  468.7 39.1 %psum.95 = f32[256,32]{0,1:T(8,128)S(1)} all-reduce(f32[256,32]{0,1:T(8,128)S(1)} %psum.94), channel_id=1, replica_groups=mesh['tok_0'=4,'tok_1'=16,'blk_0'=4,'blk_1'=2] {'tok_1'}, use_global_device_ids=true, to_apply=%region_15.18 | all-reduce | flops 8192 | bytes 65536 | tf_op jit(solution)/shard_map/psum | solution.py:37
  508.5 21.8 %all-to-all-start.5 = ((f32[8,256,32]{1,2,0:T(8,128)}), f32[8,256,32]{1,2,0:T(8,128)S(1)}, u32[]{:S(2)}, u32[]{:S(2)}) async-start(f32[8,256,32]{1,2,0:T(8,128)} %broadcast_in_dim.83), calls=%async_computation.5 | async-start | bytes 524288 | tf_op jit(solution)/shard_map/all_to_all | solution.py:21
  530.2 6.5 %all-to-all-done.5 = f32[8,256,32]{1,2,0:T(8,128)S(1)} async-done(((f32[8,256,32]{1,2,0:T(8,128)}), f32[8,256,32]{1,2,0:T(8,128)S(1)}, u32[]{:S(2)}, u32[]{:S(2)}) %all-to-all-start.5) | async-done | bytes 262176 | tf_op jit(solution)/shard_map/all_to_all | solution.py:21
  (60 shorter events, 34.9 us)
Async XLA Ops:
  0.0 25.4 %copy-start = (bf16[256,256]{1,0:T(8,128)(2,1)S(1)}, bf16[256,256]{1,0:T(8,128)(2,1)}, u32[]{:S(2)}) copy-start(bf16[256,256]{1,0:T(8,128)(2,1)} %param.4) | copy-start | bytes 393220
  27.1 106.7 %all-to-all-start.1 = ((f32[256,64,32]{0,2,1:T(8,128)}), f32[256,64,32]{0,2,1:T(8,128)S(1)}, u32[]{:S(2)}, u32[]{:S(2)}) async-start(f32[256,64,32]{0,2,1:T(8,128)} %fusion.10), calls=%async_computation.1 | async-start | bytes 4194304 | tf_op jit(solution)/shard_map/all_to_all | solution.py:54
  246.3 27.3 %all-to-all-start.2 = ((f32[8,256,32]{1,2,0:T(8,128)}), f32[8,256,32]{1,2,0:T(8,128)S(1)}, u32[]{:S(2)}, u32[]{:S(2)}) async-start(f32[8,256,32]{1,2,0:T(8,128)} %broadcast_in_dim.76), calls=%async_computation.2 | async-start | bytes 524288 | tf_op jit(solution)/shard_map/all_to_all | solution.py:21
  333.4 28.2 %all-to-all-start.3 = ((f32[8,256,32]{1,2,0:T(8,128)}), f32[8,256,32]{1,2,0:T(8,128)S(1)}, u32[]{:S(2)}, u32[]{:S(2)}) async-start(f32[8,256,32]{1,2,0:T(8,128)} %broadcast_in_dim.78), calls=%async_computation.3 | async-start | bytes 524288 | tf_op jit(solution)/shard_map/all_to_all | solution.py:21
  420.4 28.2 %all-to-all-start.4 = ((f32[8,256,32]{1,2,0:T(8,128)}), f32[8,256,32]{1,2,0:T(8,128)S(1)}, u32[]{:S(2)}, u32[]{:S(2)}) async-start(f32[8,256,32]{1,2,0:T(8,128)} %broadcast_in_dim.81), calls=%async_computation.4 | async-start | bytes 524288 | tf_op jit(solution)/shard_map/all_to_all | solution.py:21
  508.5 28.2 %all-to-all-start.5 = ((f32[8,256,32]{1,2,0:T(8,128)}), f32[8,256,32]{1,2,0:T(8,128)S(1)}, u32[]{:S(2)}, u32[]{:S(2)}) async-start(f32[8,256,32]{1,2,0:T(8,128)} %broadcast_in_dim.83), calls=%async_computation.5 | async-start | bytes 524288 | tf_op jit(solution)/shard_map/all_to_all | solution.py:21
where the time goes:
time: 546 us; the launch traced here: 545 us
  blocking collectives  288 us (53%)
  waiting for transfers between devices  118 us (22%)
  starting transfers between devices  101 us (18%)
  other arithmetic  27.9 us (5%)
    psum x8, blocking collectives, spread(): x = lax.psum(x, axis)  204 us
    all_to_all x1, waiting for transfers between devices, shards(): lax.all_to_all(partial_rows, TOK, split_axis=1, concat_axis=0, tiled=True)  91.9 us
    all_to_all x4, starting transfers between devices, from_everyone(): lax.all_to_all(jnp.broadcast_to(x[None], (length, *x.shape)), axis, 0, 0,...  86 us
    psum x4, blocking collectives, over_axes(): x = lax.psum(x, axis)  59.8 us
    all_to_all x4, waiting for transfers between devices, from_everyone(): lax.all_to_all(jnp.broadcast_to(x[None], (length, *x.shape)), axis, 0, 0,...  26 us
    all_to_all x1, blocking collectives, from_everyone(): lax.all_to_all(jnp.broadcast_to(x[None], (length, *x.shape)), axis, 0, 0,...  24.2 us
    all_to_all x1, starting transfers between devices, shards(): lax.all_to_all(partial_rows, TOK, split_axis=1, concat_axis=0, tiled=True)  14.8 us
    another operation x12, other arithmetic, shards(): factor = jnp.linalg.cholesky(pivot_block)  14.4 us
  transfers between devices with their start and end apart: 5, of which 5 were waited for; matrix products, arithmetic and copies ran while one was open for 0% of the time, Pallas kernels for 0%

commit v1 on v0

v1 whole, which is shorter than its diff:
```python
import jax
import jax.numpy as jnp
from jax import lax
from jax.experimental import pallas as pl
from jax.experimental.pallas import tpu as pltpu
from jax.sharding import Mesh
from jax.sharding import PartitionSpec as P

MESH = pl.DeviceIdType.MESH
F32 = jnp.float32
BF16 = jnp.bfloat16
NX, NZ, NY, NC = 4, 16, 4, 2
BLOCK = 256
PANEL = 128
SLICE = BLOCK // NX
FULL = BLOCK * NY * NC
TOKENS = BLOCK * NX * NZ
SCALE = 2.0 / TOKENS


def wait(ref, sem):
    pltpu.make_async_copy(ref, ref, sem).wait()


def send(src, dst, send_sem, recv_sem, device):
    pltpu.make_async_remote_copy(
        src_ref=src,
        dst_ref=dst,
        send_sem=send_sem,
        recv_sem=recv_sem,
        device_id=device,
        device_id_type=MESH,
    ).start()


def exchange(a_ref, f_out, rows_out, cols_out, pivot_out, trace_out, feats, slices, partial, inbox, total, tall,
             rows, cols, pivot, owned, tz, ty, tq, tr,
             g1_s, g1_r, sib_s, sib_r, sl_s, sl_r, z_s, z_r, tz_s, tz_r, ty_s, ty_r, p1_s, p1_r,
             rows_s, rows_r, cols_s, cols_r, piv_s, piv_r, own_s, own_r):
    x, z, y, c = (lax.axis_index(name) for name in ("x", "z", "y", "c"))
    other = 1 - c
    mine = pl.ds(pl.multiple_of(x * SLICE, SLICE), SLICE)

    feats[c, x] = a_ref[...].T
    for d in (1, 3, 2):
        send(feats.at[c, x], feats.at[c, x], g1_s.at[d], g1_r.at[x], (lax.rem(x + d, NX), z, y, c))

    def relay(piece):
        send(feats.at[c, piece], feats.at[c, piece], sib_s.at[piece], sib_r.at[piece], (x, z, y, other))
        for target in range(1, NY):
            @pl.when(target > y)
            def _():
                send(feats.at[c, piece, mine], slices.at[y, piece], sl_s.at[target, piece], sl_r.at[y, piece],
                     (x, z, target, c))
        slices[y, piece] = feats[c, piece, mine]

    relay(x)
    for d in (1, 3, 2):
        piece = lax.rem(x + d, NX)
        wait(feats.at[c, piece], g1_r.at[piece])
        relay(piece)
    for piece in range(NX):
        wait(feats.at[other, piece], sib_r.at[piece])

    for source in range(NY):
        @pl.when(source <= y)
        def _():
            @pl.when(source < y)
            def _():
                for piece in range(NX):
                    wait(slices.at[source, piece], sl_r.at[source, piece])
            for half in range(NC):
                acc = jnp.zeros((SLICE, BLOCK), F32)
                for piece in range(NX):
                    acc += lax.dot_general(slices[source, piece], feats[half, piece], (((1,), (1,)), ((), ())),
                                           preferred_element_type=F32)
                for s in range(SLICE // 8):
                    partial[source, NC * s + half] = acc[8 * s:8 * s + 8]

            @pl.loop(1, NZ)
            def _(d):
                target = lax.rem(z + d, NZ)
                send(partial.at[source, target], inbox.at[source, z], z_s.at[source], z_r.at[source], (x, target, y, c))
            pltpu.make_async_copy(partial.at[source, z], inbox.at[source, z], z_r.at[source]).start()
        if source == 0:
            acc = jnp.zeros((8, 128), F32)
            for half in range(NC):
                for piece in range(NX):
                    v = feats[half, piece].astype(F32)
                    v = jnp.sum((v * v).reshape(BLOCK // 8, 8, BLOCK), axis=0)
                    acc += v[:, :128] + v[:, 128:]
            tq[...] = acc

            @pl.loop(1, NZ)
            def _(d):
                target = lax.rem(z + d, NZ)
                send(tq, tz.at[z], tz_s, tz_r, (x, target, y, c))
            pltpu.make_async_copy(tq, tz.at[z], tz_r).start()

    panel = jnp.logical_and(x < 2, c == 0)
    zs, zc = z // NC, lax.rem(z, NC)
    wait(inbox.at[0], z_r.at[0])
    total[0] = jnp.sum(inbox[0], axis=0)

    @pl.when(panel)
    def _():
        @pl.loop(1, NZ)
        def _(d):
            target = lax.rem(z + d, NZ)
            send(total.at[0], tall.at[zc, zs], p1_s, p1_r, (x, target, y, c))
        pltpu.make_async_copy(total.at[0], tall.at[zc, zs], p1_r).start()

    wait(tz, tz_r)
    tr[...] = jnp.sum(tz[...], axis=0)

    @pl.loop(1, NY)
    def _(d):
        send(tr, ty.at[y], ty_s, ty_r, (x, z, lax.rem(y + d, NY), c))
    pltpu.make_async_copy(tr, ty.at[y], ty_r).start()

    def to_owner(source):
        owner_z = 8 * c + 2 * x + zs // 4
        local = jnp.logical_and(jnp.logical_and(source == x, owner_z == z), zc == c)
        slot = owned.at[lax.rem(zs, 4)]

        @pl.when(jnp.logical_not(local))
        def _():
            send(total.at[source], slot, own_s.at[source], own_r, (source, owner_z, y, zc))

        @pl.when(local)
        def _():
            pltpu.make_async_copy(total.at[source], slot, own_r).start()

    def owner_sent(source):
        owner_z = 8 * c + 2 * x + zs // 4
        local = jnp.logical_and(jnp.logical_and(source == x, owner_z == z), zc == c)

        @pl.when(jnp.logical_not(local))
        def _():
            wait(total.at[source], own_s.at[source])

    to_owner(0)
    for source in range(1, NY):
        @pl.when(source <= y)
        def _():
            wait(inbox.at[source], z_r.at[source])
            total[source] = jnp.sum(inbox[source], axis=0)
            to_owner(source)

    col_half = z // 8
    col_lanes = pl.ds(pl.multiple_of(lax.rem(z, 8) // 4 * 128, 128), 128)

    def spread(src, dst, sems, recv, count, place):
        @pl.loop(0, count)
        def _(i):
            tx, ty_, tc = place(i)
            here = jnp.logical_and(jnp.logical_and(tx == x, ty_ == y), tc == c)

            @pl.when(here)
            def _():
                pltpu.make_async_copy(src, dst, recv).start()

            @pl.when(jnp.logical_not(here))
            def _():
                send(src, dst, sems.at[i], recv, (tx, z, ty_, tc))

    def spread_done(src, sems, count, place):
        @pl.loop(0, count)
        def _(i):
            tx, ty_, tc = place(i)
            here = jnp.logical_and(jnp.logical_and(tx == x, ty_ == y), tc == c)

            @pl.when(jnp.logical_not(here))
            def _():
                wait(src, sems.at[i])

    def place_pivot(i):
        return i // 8, lax.rem(i // 2, NY), lax.rem(i, NC)

    def place_cols(i):
        return y, i // 2, lax.rem(i, NC)

    def place_rows(half):
        return lambda i: (i, y, half)

    pivot_src = tall.at[0, :, :, pl.ds(0, 128)]
    cols_src = tall.at[col_half, :, :, col_lanes]

    @pl.when(panel)
    def _():
        wait(tall, p1_r)

        @pl.when(y == 0)
        def _():
            spread(pivot_src, pivot.at[x], piv_s, piv_r, 32, place_pivot)
        spread(cols_src, cols.at[x], cols_s, cols_r, 8, place_cols)
        for half in range(NC):
            spread(tall.at[half], rows.at[x], rows_s.at[half], rows_r, NX, place_rows(half))

    wait(pivot, piv_r)
    wait(cols, cols_r)
    wait(rows, rows_r)
    wait(ty, ty_r)
    pivot_out[...] = pivot[...].reshape(PANEL, PANEL)
    cols_out[...] = cols[...].reshape(PANEL, PANEL)
    rows_out[...] = rows[...].reshape(PANEL, BLOCK)
    trace_out[...] = jnp.sum(ty[...], axis=0)

    @pl.when(x <= y)
    def _():
        wait(owned, own_r)
    f_out[...] = owned[...].reshape(32, BLOCK)

    for d in (1, 3, 2):
        wait(feats.at[c, x], g1_s.at[d])
    for piece in range(NX):
        wait(feats.at[c, piece], sib_s.at[piece])
        for target in range(1, NY):
            @pl.when(target > y)
            def _():
                wait(slices.at[y, piece], sl_s.at[target, piece])
    owner_sent(0)
    wait(partial.at[0, pl.ds(0, NZ - 1)], z_s.at[0])
    for source in range(1, NY):
        @pl.when(source <= y)
        def _():
            wait(partial.at[source, pl.ds(0, NZ - 1)], z_s.at[source])
            owner_sent(source)
    wait(tz.at[pl.ds(0, NZ - 1)], tz_s)
    wait(ty.at[pl.ds(0, NY - 1)], ty_s)

    @pl.when(panel)
    def _():
        for _ in range(1):
            wait(inbox.at[0, pl.ds(0, NZ - 1)], p1_s)

        @pl.when(y == 0)
        def _():
            spread_done(pivot_src, piv_s, 32, place_pivot)
        spread_done(cols_src, cols_s, 8, place_cols)
        for half in range(NC):
            spread_done(tall.at[half], rows_s.at[half], NX, place_rows(half))


def gathered(a):
    dma = pltpu.SemaphoreType.DMA
    vmem = pl.BlockSpec(memory_space=pltpu.VMEM)
    return pl.pallas_call(
        exchange,
        out_shape=[
            jax.ShapeDtypeStruct((32, BLOCK), F32),
            jax.ShapeDtypeStruct((PANEL, BLOCK), F32),
            jax.ShapeDtypeStruct((PANEL, PANEL), F32),
            jax.ShapeDtypeStruct((PANEL, PANEL), F32),
            jax.ShapeDtypeStruct((8, 128), F32),
        ],
        in_specs=[vmem],
        out_specs=[vmem] * 5,
        scratch_shapes=[
            pltpu.VMEM((NC, NX, BLOCK, BLOCK), BF16),
            pltpu.VMEM((NY, NX, SLICE, BLOCK), BF16),
            pltpu.VMEM((NY, NZ, 8, BLOCK), F32),
            pltpu.VMEM((NY, NZ, 8, BLOCK), F32),
            pltpu.VMEM((NY, 8, BLOCK), F32),
            pltpu.VMEM((NC, 8, 8, BLOCK), F32),
            pltpu.VMEM((2, 8, 8, BLOCK), F32),
            pltpu.VMEM((2, 8, 8, 128), F32),
            pltpu.VMEM((2, 8, 8, 128), F32),
            pltpu.VMEM((4, 8, BLOCK), F32),
            pltpu.VMEM((NZ, 8, 128), F32),
            pltpu.VMEM((NY, 8, 128), F32),
            pltpu.VMEM((8, 128), F32),
            pltpu.VMEM((8, 128), F32),
            dma((NX,)), dma((NX,)),
            dma((NX,)), dma((NX,)),
            dma((NY, NX)), dma((NY, NX)),
            dma((NY,)), dma((NY,)),
            dma(()), dma(()),
            dma(()), dma(()),
            dma(()), dma(()),
            dma((NC, NX)), dma(()),
            dma((8,)), dma(()),
            dma((32,)), dma(()),
            dma((NY,)), dma(()),
        ],
        compiler_params=pltpu.CompilerParams(has_side_effects=True),
    )(a)


def finish(f_ref, rows_ref, cols_ref, pivot_ref, trace_ref, out_ref, both):
    x, z, y, c = (lax.axis_index(name) for name in ("x", "z", "y", "c"))
    damp = jnp.sum(trace_ref[...], keepdims=True) * (SCALE * 0.01 / FULL)
    lane = lax.broadcasted_iota(jnp.int32, (8, PANEL), 1)
    sub = lax.broadcasted_iota(jnp.int32, (8, PANEL), 0)
    groups = []
    for g in range(PANEL // 8):
        diag = lane == sub + 8 * g
        left = pivot_ref[8 * g:8 * g + 8, :] * SCALE + jnp.where(diag, damp, 0.0)
        groups.append([left, jnp.where(diag, 1.0, 0.0).astype(F32)])
    for k in range(PANEL):
        g0, r0 = k // 8, k % 8
        left, right = groups[g0][0][r0:r0 + 1], groups[g0][1][r0:r0 + 1]
        inv = 1.0 / left[:, k:k + 1]
        left, right = left * inv, right * inv
        for g in range(g0, PANEL // 8):
            mult = groups[g][0][:, k:k + 1]
            if g == g0:
                if r0 == 7:
                    continue
                mult = jnp.where(sub[:, :1] > r0, mult, 0.0)
            groups[g] = [groups[g][0] - mult * left, groups[g][1] - mult * right]
    for g in range(PANEL // 8):
        diag = jnp.sum(jnp.where(lane == sub + 8 * g, groups[g][0], 0.0), axis=1, keepdims=True)
        both[8 * g:8 * g + 8, :] = groups[g][1] * lax.rsqrt(diag)
    inverse = both[...]
    ids = lax.broadcasted_iota(jnp.int32, (PANEL, BLOCK), 0)
    row0 = (y * NC + c) * BLOCK
    row_ids = row0 + lax.broadcasted_iota(jnp.int32, (PANEL, BLOCK), 1)
    rows = rows_ref[...] * SCALE + jnp.where(ids == row_ids, damp, 0.0)
    highest = lax.Precision.HIGHEST
    rows = jnp.dot(inverse, rows, precision=highest, preferred_element_type=F32)
    cols = jnp.dot(inverse, cols_ref[...] * SCALE, precision=highest, preferred_element_type=F32)
    both_rows = lax.dot_general(cols, rows, (((0,), (0,)), ((), ())), precision=highest, preferred_element_type=F32)
    strip0 = (x * NZ + z) * 32
    leading = strip0 < PANEL
    picked = jnp.where(leading, rows, both_rows)
    wide = jnp.zeros((32, BLOCK), F32)
    for q in range(4):
        wide = jnp.where(lax.rem(z, 4) == q, picked[32 * q:32 * q + 32], wide)
    col_ids = strip0 + lax.broadcasted_iota(jnp.int32, (32, BLOCK), 0)
    row_ids = row0 + lax.broadcasted_iota(jnp.int32, (32, BLOCK), 1)
    schur = f_ref[...] * SCALE + jnp.where(col_ids == row_ids, damp, 0.0) - wide
    wide = jnp.where(leading, wide, schur)
    out_ref[...] = jnp.where(row_ids >= col_ids, wide, 0.0).T


def shards(a):
    parts = gathered(a)
    vmem = pl.BlockSpec(memory_space=pltpu.VMEM)
    return pl.pallas_call(
        finish,
        out_shape=jax.ShapeDtypeStruct((BLOCK, 32), F32),
        in_specs=[vmem] * 5,
        out_specs=vmem,
        scratch_shapes=[pltpu.VMEM((PANEL, PANEL), F32)],
    )(*parts)


def solution(mesh):
    finer = Mesh(mesh.devices.reshape(NX, NZ, NY, NC), ("x", "z", "y", "c"))
    return jax.shard_map(
        shards, mesh=finer, in_specs=(P(("x", "z"), ("y", "c")),), out_specs=P(("y", "c"), ("x", "z")), check_vma=False
    )
```

time: 546 us -> 100 us (0.18)
  the two profiles are of different devices: /device:TPU:1 before, /device:TPU:31 now
where the time goes in v1:
time: 100 us
  Pallas kernels  98.6 us (99%)
  local copies, waits for them, and re-layouts  1.59 us (2%)
    pallas_call x1, Pallas kernels, gathered(): pl.pallas_call(exchange, out_shape=[jax.ShapeDtypeStruct((32, BLOCK), F32...  85.3 us
    pallas_call x1, Pallas kernels, shards(): pl.pallas_call(finish, out_shape=jax.ShapeDtypeStruct((BLOCK, 32), F32),...  13.3 us

profile of v1, /device:TPU:31, one launch (start us, length us, event | category | flops | bytes accessed | tf_op | source)
XLA Modules:
  0.0 100.2 jit_solution(4530227774155378067)
XLA Ops:
  0.0 85.3 %shard_map.17 = (f32[32,256]{1,0:T(8,128)}, f32[128,256]{1,0:T(8,128)}, f32[128,128]{1,0:T(8,128)}, f32[128,128]{1,0:T(8,128)}, f32[8,128]{1,0:T(8,128)}) custom-call(bf16[256,256]{1,0:T(8,128)(2,1)} %a_ref.1), custom_call_target="tpu_custom_call" | custom-call | tf_op jit(solution)/shard_map/pallas_call | solution.py:248
  85.3 13.3 %shard_map.18 = f32[256,32]{1,0:T(8,128)} custom-call(f32[32,256]{1,0:T(8,128)} %get-tuple-element.10.f_ref, f32[128,256]{1,0:T(8,128)} %get-tuple-element.11.rows_ref, f32[128,128]{1,0:T(8,128)} %get-tuple-element.12.cols_ref, f32[128,128]{1,0:T(8,128)} %get-tuple-element.13.pivot_ref, f32[8,128]{1,0:T(8,128)} %get-tuple-element.14.trace_ref), custom_call_target="tpu_custom_call" | custom-call | tf_op jit(solution)/shard_map/pallas_call | solution.py:340
  98.6 1.6 %copy.2 = f32[256,32]{0,1:T(8,128)} copy(f32[256,32]{1,0:T(8,128)} %shard_map.18) | data formatting | bytes 65536 | tf_op jit(solution)/shard_map/pallas_call | solution.py:340

commit v2 on v1

v2 whole, which is shorter than its diff:
```python
import jax
import jax.numpy as jnp
from jax import lax
from jax.experimental import pallas as pl
from jax.experimental.pallas import tpu as pltpu
from jax.sharding import Mesh
from jax.sharding import PartitionSpec as P

MESH = pl.DeviceIdType.MESH
F32 = jnp.float32
BF16 = jnp.bfloat16
NX, NZ, NY, NC = 4, 16, 4, 2
BLOCK = 256
PANEL = 128
SLICE = BLOCK // NX
FULL = BLOCK * NY * NC
TOKENS = BLOCK * NX * NZ
SCALE = 2.0 / TOKENS


def wait(ref, sem):
    pltpu.make_async_copy(ref, ref, sem).wait()


def send(src, dst, send_sem, recv_sem, device):
    pltpu.make_async_remote_copy(
        src_ref=src,
        dst_ref=dst,
        send_sem=send_sem,
        recv_sem=recv_sem,
        device_id=device,
        device_id_type=MESH,
    ).start()


def eliminate(groups, first, last, sub):
    for k in range(first, last):
        g0, r0 = k // 8, k % 8
        left, right = groups[g0][0][r0:r0 + 1], groups[g0][1][r0:r0 + 1]
        inv = 1.0 / left[:, k:k + 1]
        left, right = left * inv, right * inv
        for g in range(g0, PANEL // 8):
            mult = groups[g][0][:, k:k + 1]
            if g == g0:
                if r0 == 7:
                    continue
                mult = jnp.where(sub[:, :1] > r0, mult, 0.0)
            groups[g] = [groups[g][0] - mult * left, groups[g][1] - mult * right]


def exchange(a_ref, out_ref, feats, slices, partial, inbox, total, tall,
             rows, cols, pivot, owned, tz, ty, tq, tr, square,
             g1_s, g1_r, sib_s, sib_r, sl_s, sl_r, z_s, z_r, tz_s, tz_r, ty_s, ty_r, p1_s, p1_r,
             rows_s, rows_r, cols_s, cols_r, piv_s, piv_r, own_s, own_r):
    x, z, y, c = (lax.axis_index(name) for name in ("x", "z", "y", "c"))
    other = 1 - c
    mine = pl.ds(pl.multiple_of(x * SLICE, SLICE), SLICE)

    barrier = pltpu.get_barrier_semaphore()

    @pl.loop(1, NX * NY * NC)
    def _(i):
        there = (lax.rem(x + i // (NY * NC), NX), z, lax.rem(y + i // NC, NY), lax.rem(c + i, NC))
        pl.semaphore_signal(barrier, inc=1, device_id=there, device_id_type=MESH)

    @pl.loop(1, NZ)
    def _(d):
        there = (x, lax.rem(z + d, NZ), y, c)
        pl.semaphore_signal(barrier, inc=1, device_id=there, device_id_type=MESH)

    feats[c, x] = a_ref[...].T
    pl.semaphore_wait(barrier, NX * NY * NC - 1 + NZ - 1)
    for d in (1, 3, 2):
        send(feats.at[c, x], feats.at[c, x], g1_s.at[d], g1_r.at[x], (lax.rem(x + d, NX), z, y, c))

    def relay(piece):
        send(feats.at[c, piece], feats.at[c, piece], sib_s.at[piece], sib_r.at[piece], (x, z, y, other))
        for target in range(1, NY):
            @pl.when(target > y)
            def _():
                send(feats.at[c, piece, mine], slices.at[y, piece], sl_s.at[target, piece], sl_r.at[y, piece],
                     (x, z, target, c))
        slices[y, piece] = feats[c, piece, mine]

    relay(x)
    for d in (1, 3, 2):
        piece = lax.rem(x + d, NX)
        wait(feats.at[c, piece], g1_r.at[piece])
        relay(piece)
    for piece in range(NX):
        wait(feats.at[other, piece], sib_r.at[piece])

    def multiply(source):
        for half in range(NC):
            acc = jnp.zeros((SLICE, BLOCK), F32)
            for piece in range(NX):
                acc += lax.dot_general(slices[source, piece], feats[half, piece], (((1,), (1,)), ((), ())),
                                       preferred_element_type=F32)
            for s in range(SLICE // 8):
                partial[source, NC * s + half] = acc[8 * s:8 * s + 8]

    def reduce_to_peers(source):
        @pl.loop(1, NZ)
        def _(d):
            target = lax.rem(z + d, NZ)
            send(partial.at[source, target], inbox.at[source, z], z_s.at[source], z_r.at[source], (x, target, y, c))
        pltpu.make_async_copy(partial.at[source, z], inbox.at[source, z], z_r.at[source]).start()

    def arrived(source):
        @pl.when(source < y)
        def _():
            for piece in range(NX):
                wait(slices.at[source, piece], sl_r.at[source, piece])

    panel = jnp.logical_and(x < 2, c == 0)
    zs, zc = z // NC, lax.rem(z, NC)

    arrived(0)
    multiply(0)
    reduce_to_peers(0)
    acc = jnp.zeros((8, 128), F32)
    for half in range(NC):
        for piece in range(NX):
            v = feats[half, piece].astype(F32)
            v = jnp.sum((v * v).reshape(BLOCK // 8, 8, BLOCK), axis=0)
            acc += v[:, :128] + v[:, 128:]
    tq[...] = acc

    @pl.loop(1, NZ)
    def _(d):
        target = lax.rem(z + d, NZ)
        send(tq, tz.at[z], tz_s, tz_r, (x, target, y, c))
    pltpu.make_async_copy(tq, tz.at[z], tz_r).start()

    for source in range(1, NY):
        @pl.when(source <= y)
        def _():
            arrived(source)
            multiply(source)

            @pl.when(x >= 2)
            def _():
                reduce_to_peers(source)

    wait(inbox.at[0], z_r.at[0])
    total[0] = jnp.sum(inbox[0], axis=0)

    @pl.when(panel)
    def _():
        @pl.loop(1, NZ)
        def _(d):
            target = lax.rem(z + d, NZ)
            send(total.at[0], tall.at[zc, zs], p1_s, p1_r, (x, target, y, c))
        pltpu.make_async_copy(total.at[0], tall.at[zc, zs], p1_r).start()

    wait(tz, tz_r)
    tr[...] = jnp.sum(tz[...], axis=0)

    @pl.loop(1, NY)
    def _(d):
        send(tr, ty.at[y], ty_s, ty_r, (x, z, lax.rem(y + d, NY), c))
    pltpu.make_async_copy(tr, ty.at[y], ty_r).start()

    @pl.when(x < 2)
    def _():
        for source in range(1, NY):
            @pl.when(source <= y)
            def _():
                reduce_to_peers(source)

    def to_owner(source):
        owner_z = 8 * c + 2 * x + zs // 4
        local = jnp.logical_and(jnp.logical_and(source == x, owner_z == z), zc == c)
        slot = owned.at[lax.rem(zs, 4)]

        @pl.when(jnp.logical_not(local))
        def _():
            send(total.at[source], slot, own_s.at[source], own_r, (source, owner_z, y, zc))

        @pl.when(local)
        def _():
            pltpu.make_async_copy(total.at[source], slot, own_r).start()

    def owner_sent(source):
        owner_z = 8 * c + 2 * x + zs // 4
        local = jnp.logical_and(jnp.logical_and(source == x, owner_z == z), zc == c)

        @pl.when(jnp.logical_not(local))
        def _():
            wait(total.at[source], own_s.at[source])

    to_owner(0)

    col_half = z // 8
    col_lanes = pl.ds(pl.multiple_of(lax.rem(z, 8) // 4 * 128, 128), 128)

    def spread(src, dst, sems, recv, count, place):
        @pl.loop(0, count)
        def _(i):
            tx, ty_, tc = place(i)
            here = jnp.logical_and(jnp.logical_and(tx == x, ty_ == y), tc == c)

            @pl.when(here)
            def _():
                pltpu.make_async_copy(src, dst, recv).start()

            @pl.when(jnp.logical_not(here))
            def _():
                send(src, dst, sems.at[i], recv, (tx, z, ty_, tc))

    def spread_done(src, sems, count, place):
        @pl.loop(0, count)
        def _(i):
            tx, ty_, tc = place(i)
            here = jnp.logical_and(jnp.logical_and(tx == x, ty_ == y), tc == c)

            @pl.when(jnp.logical_not(here))
            def _():
                wait(src, sems.at[i])

    def place_pivot(i):
        return i // 8, lax.rem(i // 2, NY), lax.rem(i, NC)

    def place_cols(i):
        return y, i // 2, lax.rem(i, NC)

    def place_rows(half):
        return lambda i: (i, y, half)

    pivot_src = tall.at[0, :, :, pl.ds(0, 128)]
    cols_src = tall.at[col_half, :, :, col_lanes]

    @pl.when(panel)
    def _():
        wait(tall, p1_r)

        @pl.when(y == 0)
        def _():
            spread(pivot_src, pivot.at[x], piv_s, piv_r, 32, place_pivot)
        spread(cols_src, cols.at[x], cols_s, cols_r, 8, place_cols)
        for half in range(NC):
            spread(tall.at[half], rows.at[x], rows_s.at[half], rows_r, NX, place_rows(half))

    wait(pivot, piv_r)
    wait(ty, ty_r)
    damp = jnp.sum(jnp.sum(ty[...], axis=0), keepdims=True) * (SCALE * 0.01 / FULL)
    lane = lax.broadcasted_iota(jnp.int32, (8, PANEL), 1)
    sub = lax.broadcasted_iota(jnp.int32, (8, PANEL), 0)
    groups = []
    for g in range(PANEL // 8):
        diag = lane == sub + 8 * g
        left = pivot[g // 8, g % 8] * SCALE + jnp.where(diag, damp, 0.0)
        groups.append([left, jnp.where(diag, 1.0, 0.0).astype(F32)])
    eliminate(groups, 0, PANEL // 2, sub)
    for g in range(PANEL // 8):
        square[g, 0] = groups[g][0]
        square[g, 1] = groups[g][1]
    for source in range(1, NY):
        @pl.when(source <= y)
        def _():
            wait(inbox.at[source], z_r.at[source])
            total[source] = jnp.sum(inbox[source], axis=0)
            to_owner(source)
    groups = [[square[g, 0], square[g, 1]] for g in range(PANEL // 8)]
    eliminate(groups, PANEL // 2, PANEL, sub)
    scaled = []
    for g in range(PANEL // 8):
        diag = jnp.sum(jnp.where(lane == sub + 8 * g, groups[g][0], 0.0), axis=1, keepdims=True)
        scaled.append(groups[g][1] * lax.rsqrt(diag))
    inverse = jnp.concatenate(scaled, axis=0)
    wait(cols, cols_r)
    wait(rows, rows_r)
    ids = lax.broadcasted_iota(jnp.int32, (PANEL, BLOCK), 0)
    row0 = (y * NC + c) * BLOCK
    row_ids = row0 + lax.broadcasted_iota(jnp.int32, (PANEL, BLOCK), 1)
    right = rows[...].reshape(PANEL, BLOCK) * SCALE + jnp.where(ids == row_ids, damp, 0.0)
    highest = lax.Precision.HIGHEST
    right = jnp.dot(inverse, right, precision=highest, preferred_element_type=F32)
    left = jnp.dot(inverse, cols[...].reshape(PANEL, PANEL) * SCALE, precision=highest, preferred_element_type=F32)
    update = lax.dot_general(left, right, (((0,), (0,)), ((), ())), precision=highest, preferred_element_type=F32)
    strip0 = (x * NZ + z) * 32
    leading = strip0 < PANEL
    picked = jnp.where(leading, right, update)
    wide = jnp.zeros((32, BLOCK), F32)
    for q in range(4):
        wide = jnp.where(lax.rem(z, 4) == q, picked[32 * q:32 * q + 32], wide)
    col_ids = strip0 + lax.broadcasted_iota(jnp.int32, (32, BLOCK), 0)
    row_ids = row0 + lax.broadcasted_iota(jnp.int32, (32, BLOCK), 1)

    @pl.when(x <= y)
    def _():
        wait(owned, own_r)
    schur = owned[...].reshape(32, BLOCK) * SCALE + jnp.where(col_ids == row_ids, damp, 0.0) - wide
    wide = jnp.where(leading, wide, schur)
    out_ref[...] = jnp.where(row_ids >= col_ids, wide, 0.0)

    for d in (1, 3, 2):
        wait(feats.at[c, x], g1_s.at[d])
    for piece in range(NX):
        wait(feats.at[c, piece], sib_s.at[piece])
        for target in range(1, NY):
            @pl.when(target > y)
            def _():
                wait(slices.at[y, piece], sl_s.at[target, piece])
    owner_sent(0)
    wait(partial.at[0, pl.ds(0, NZ - 1)], z_s.at[0])
    for source in range(1, NY):
        @pl.when(source <= y)
        def _():
            wait(partial.at[source, pl.ds(0, NZ - 1)], z_s.at[source])
            owner_sent(source)
    wait(tz.at[pl.ds(0, NZ - 1)], tz_s)
    wait(ty.at[pl.ds(0, NY - 1)], ty_s)

    @pl.when(panel)
    def _():
        for _ in range(1):
            wait(inbox.at[0, pl.ds(0, NZ - 1)], p1_s)

        @pl.when(y == 0)
        def _():
            spread_done(pivot_src, piv_s, 32, place_pivot)
        spread_done(cols_src, cols_s, 8, place_cols)
        for half in range(NC):
            spread_done(tall.at[half], rows_s.at[half], NX, place_rows(half))


def gathered(a):
    dma = pltpu.SemaphoreType.DMA
    vmem = pl.BlockSpec(memory_space=pltpu.VMEM)
    return pl.pallas_call(
        exchange,
        out_shape=jax.ShapeDtypeStruct((32, BLOCK), F32),
        in_specs=[vmem],
        out_specs=vmem,
        scratch_shapes=[
            pltpu.VMEM((NC, NX, BLOCK, BLOCK), BF16),
            pltpu.VMEM((NY, NX, SLICE, BLOCK), BF16),
            pltpu.VMEM((NY, NZ, 8, BLOCK), F32),
            pltpu.VMEM((NY, NZ, 8, BLOCK), F32),
            pltpu.VMEM((NY, 8, BLOCK), F32),
            pltpu.VMEM((NC, 8, 8, BLOCK), F32),
            pltpu.VMEM((2, 8, 8, BLOCK), F32),
            pltpu.VMEM((2, 8, 8, 128), F32),
            pltpu.VMEM((2, 8, 8, 128), F32),
            pltpu.VMEM((4, 8, BLOCK), F32),
            pltpu.VMEM((NZ, 8, 128), F32),
            pltpu.VMEM((NY, 8, 128), F32),
            pltpu.VMEM((8, 128), F32),
            pltpu.VMEM((8, 128), F32),
            pltpu.VMEM((PANEL // 8, 2, 8, PANEL), F32),
            dma((NX,)), dma((NX,)),
            dma((NX,)), dma((NX,)),
            dma((NY, NX)), dma((NY, NX)),
            dma((NY,)), dma((NY,)),
            dma(()), dma(()),
            dma(()), dma(()),
            dma(()), dma(()),
            dma((NC, NX)), dma(()),
            dma((8,)), dma(()),
            dma((32,)), dma(()),
            dma((NY,)), dma(()),
        ],
        compiler_params=pltpu.CompilerParams(collective_id=0, has_side_effects=True),
    )(a)


def shards(a):
    return gathered(a).T


def solution(mesh):
    finer = Mesh(mesh.devices.reshape(NX, NZ, NY, NC), ("x", "z", "y", "c"))
    return jax.shard_map(
        shards, mesh=finer, in_specs=(P(("x", "z"), ("y", "c")),), out_specs=P(("y", "c"), ("x", "z")), check_vma=False
    )
```

time: 100 us -> 77.1 us (0.77)
  the two profiles are of different devices: /device:TPU:31 before, /device:TPU:26 now
where the time goes in v2:
time: 77.1 us; the launch traced here: 76.9 us
  Pallas kernels  75.5 us (98%)
  local copies, waits for them, and re-layouts  1.38 us (2%)
    pallas_call x1, Pallas kernels, gathered(): pl.pallas_call(exchange, out_shape=jax.ShapeDtypeStruct((32, BLOCK), F32)...  75.5 us

profile of v2, /device:TPU:26, one launch (start us, length us, event | category | flops | bytes accessed | tf_op | source)
XLA Modules:
  0.0 76.9 jit_solution(12334101928624052672)
XLA Ops:
  0.0 75.5 %shard_map.17 = f32[32,256]{1,0:T(8,128)} custom-call(bf16[256,256]{1,0:T(8,128)(2,1)} %a_ref.1), custom_call_target="tpu_custom_call" | custom-call | tf_op jit(solution)/shard_map/pallas_call | solution.py:331
  75.6 1.4 %copy.3 = f32[256,32]{0,1:T(8,128)} copy(f32[256,32]{0,1:T(8,128)} %bitcast.1) | data formatting | bytes 65536

commit v3 on v2

--- a/solution.py
+++ b/solution.py
@@ -33,25 +33,54 @@
     ).start()
 
 
+def spread_rows(row):
+    return jnp.broadcast_to(row, (8, PANEL))
+
+
+def spread_lane(tile, lane):
+    return jnp.broadcast_to(tile[:, lane:lane + 1], (8, PANEL))
+
+
 def eliminate(groups, first, last, sub):
-    for k in range(first, last):
+    for k in range(first, last, 4):
         g0, r0 = k // 8, k % 8
-        left, right = groups[g0][0][r0:r0 + 1], groups[g0][1][r0:r0 + 1]
-        inv = 1.0 / left[:, k:k + 1]
-        left, right = left * inv, right * inv
-        for g in range(g0, PANEL // 8):
-            mult = groups[g][0][:, k:k + 1]
+        head = groups[g0]
+        rows = [[spread_rows(head[h][r0 + i:r0 + i + 1]) for h in range(2)] for i in range(4)]
+        dots = [[spread_lane(rows[i][0], k + j) if j >= i else None for j in range(4)] for i in range(4)]
+        mults = [[None] * 4 for _ in range(4)]
+        scaled = []
+        for i in range(4):
+            inv = 1.0 / dots[i][i]
+            for j in range(i + 1, 4):
+                mults[i][j] = dots[i][j] * inv
+            for j in range(i + 1, 4):
+                for l in range(j, 4):
+                    dots[j][l] = dots[j][l] - mults[i][j] * dots[i][l]
+                rows[j] = [rows[j][h] - mults[i][j] * rows[i][h] for h in range(2)]
+            scaled.append([rows[i][h] * inv for h in range(2)])
+        for i in (2, 1, 0):
+            for j in range(i + 1, 4):
+                scaled[i] = [scaled[i][h] - mults[i][j] * scaled[j][h] for h in range(2)]
+        for g in range(g0 if r0 == 0 else g0 + 1, PANEL // 8):
+            tile = groups[g]
+            new = list(tile)
+            for j in range(4):
+                factor = spread_lane(tile[0], k + j)
+                new = [new[h] - factor * scaled[j][h] for h in range(2)]
             if g == g0:
-                if r0 == 7:
-                    continue
-                mult = jnp.where(sub[:, :1] > r0, mult, 0.0)
-            groups[g] = [groups[g][0] - mult * left, groups[g][1] - mult * right]
+                new = [jnp.where(sub > 3, new[h], tile[h]) for h in range(2)]
+            groups[g] = new
+        for h in range(2):
+            tile = groups[g0][h]
+            for i in range(4):
+                tile = jnp.where(sub == r0 + i, rows[i][h], tile)
+            groups[g0] = [tile, groups[g0][1]] if h == 0 else [groups[g0][0], tile]
 
 
 def exchange(a_ref, out_ref, feats, slices, partial, inbox, total, tall,
              rows, cols, pivot, owned, tz, ty, tq, tr, square,
              g1_s, g1_r, sib_s, sib_r, sl_s, sl_r, z_s, z_r, tz_s, tz_r, ty_s, ty_r, p1_s, p1_r,
-             rows_s, rows_r, cols_s, cols_r, piv_s, piv_r, own_s, own_r):
+             rows_s, rows_r, cols_s, cols_r, piv_s, piv_r, own_s, own_r, move_s, move_r):
     x, z, y, c = (lax.axis_index(name) for name in ("x", "z", "y", "c"))
     other = 1 - c
     mine = pl.ds(pl.multiple_of(x * SLICE, SLICE), SLICE)
@@ -99,12 +128,72 @@
             for s in range(SLICE // 8):
                 partial[source, NC * s + half] = acc[8 * s:8 * s + 8]
 
-    def reduce_to_peers(source):
-        @pl.loop(1, NZ)
-        def _(d):
-            target = lax.rem(z + d, NZ)
-            send(partial.at[source, target], inbox.at[source, z], z_s.at[source], z_r.at[source], (x, target, y, c))
-        pltpu.make_async_copy(partial.at[source, z], inbox.at[source, z], z_r.at[source]).start()
+    moved = {2: jnp.logical_or(y == 3, jnp.logical_and(y == 2, c == 0)), 3: jnp.logical_and(y == 3, c == 0)}
+    taken = {2: jnp.logical_or(y == 0, jnp.logical_and(y == 1, c == 0)), 3: jnp.logical_and(y == 0, c == 0)}
+
+    def owner_row(k):
+        return jnp.where(taken[k], NY - 1 - y, y) if k in taken else y
+
+    def active(k):
+        own = k <= y
+        return jnp.logical_or(jnp.logical_and(own, jnp.logical_not(moved[k])), taken[k]) if k in moved else own
+
+    def halved(k):
+        return jnp.logical_and(c == 1, y == k)
+
+    def reduce_to_peers(k):
+        @pl.when(jnp.logical_not(halved(k)))
+        def _():
+            @pl.loop(1, NZ)
+            def _(d):
+                target = lax.rem(z + d, NZ)
+                send(partial.at[k, target], inbox.at[k, z], z_s.at[k], z_r.at[k], (x, target, y, c))
+            pltpu.make_async_copy(partial.at[k, z], inbox.at[k, z], z_r.at[k]).start()
+
+        @pl.when(halved(k))
+        def _():
+            @pl.loop(0, NZ // 2)
+            def _(d):
+                target = lax.rem(z + 2 * d + 1 - zc, NZ)
+
+                @pl.when(target == z)
+                def _():
+                    pltpu.make_async_copy(partial.at[k, z], inbox.at[k, z], z_r.at[k]).start()
+
+                @pl.when(target != z)
+                def _():
+                    send(partial.at[k, target], inbox.at[k, z], z_s.at[k], z_r.at[k], (x, target, y, c))
+
+    def reduced(k):
+        @pl.when(jnp.logical_and(active(k), jnp.logical_not(jnp.logical_and(halved(k), zc == 0))))
+        def _():
+            wait(inbox.at[k], z_r.at[k])
+            total[k] = jnp.sum(inbox[k], axis=0)
+            if k == 0:
+                pl.when(jnp.logical_not(panel))(lambda: to_owner(k))
+            else:
+                to_owner(k)
+
+    def sent_to_peers(k):
+        @pl.when(active(k))
+        def _():
+            @pl.when(jnp.logical_not(halved(k)))
+            def _():
+                wait(partial.at[k, pl.ds(0, NZ - 1)], z_s.at[k])
+
+            @pl.when(jnp.logical_and(halved(k), zc == 0))
+            def _():
+                wait(partial.at[k, pl.ds(0, NZ // 2)], z_s.at[k])
+
+            @pl.when(jnp.logical_and(halved(k), zc == 1))
+            def _():
+                wait(partial.at[k, pl.ds(0, NZ // 2 - 1)], z_s.at[k])
+
+    def taken_in(k):
+        if k in taken:
+            @pl.when(taken[k])
+            def _():
+                wait(partial.at[k], move_r.at[k])
 
     def arrived(source):
         @pl.when(source < y)
@@ -114,6 +203,28 @@
 
     panel = jnp.logical_and(x < 2, c == 0)
     zs, zc = z // NC, lax.rem(z, NC)
+
+    def to_owner(k):
+        owner_z = 8 * c + 2 * x + zs // 4
+        local = jnp.logical_and(jnp.logical_and(k == x, owner_z == z), jnp.logical_and(zc == c, owner_row(k) == y))
+        slot = owned.at[lax.rem(zs, 4)]
+
+        @pl.when(jnp.logical_not(local))
+        def _():
+            send(total.at[k], slot, own_s.at[k], own_r, (k, owner_z, owner_row(k), zc))
+
+        @pl.when(local)
+        def _():
+            pltpu.make_async_copy(total.at[k], slot, own_r).start()
+
+    def owner_sent(k):
+        owner_z = 8 * c + 2 * x + zs // 4
+        local = jnp.logical_and(jnp.logical_and(k == x, owner_z == z), jnp.logical_and(zc == c, owner_row(k) == y))
+        sent = jnp.logical_and(active(k), jnp.logical_not(jnp.logical_and(halved(k), zc == 0)))
+
+        @pl.when(jnp.logical_and(sent, jnp.logical_not(local)))
+        def _():
+            wait(total.at[k], own_s.at[k])
 
     arrived(0)
     multiply(0)
@@ -132,21 +243,28 @@
         send(tq, tz.at[z], tz_s, tz_r, (x, target, y, c))
     pltpu.make_async_copy(tq, tz.at[z], tz_r).start()
 
-    for source in range(1, NY):
-        @pl.when(source <= y)
-        def _():
-            arrived(source)
-            multiply(source)
-
-            @pl.when(x >= 2)
-            def _():
-                reduce_to_peers(source)
-
-    wait(inbox.at[0], z_r.at[0])
-    total[0] = jnp.sum(inbox[0], axis=0)
+    for k in (2, 3, 1):
+        @pl.when(k <= y)
+        def _():
+            arrived(k)
+            multiply(k)
+        if k in moved:
+            @pl.when(moved[k])
+            def _():
+                send(partial.at[k], partial.at[k], move_s.at[k], move_r.at[k], (x, z, NY - 1 - y, c))
+    pl.when(active(1))(lambda: reduce_to_peers(1))
+
+    @pl.when(x >= 2)
+    def _():
+        for k in (2, 3):
+            taken_in(k)
+            pl.when(active(k))(lambda: reduce_to_peers(k))
 
     @pl.when(panel)
     def _():
+        wait(inbox.at[0], z_r.at[0])
+        total[0] = jnp.sum(inbox[0], axis=0)
+
         @pl.loop(1, NZ)
         def _(d):
             target = lax.rem(z + d, NZ)
@@ -163,33 +281,12 @@
 
     @pl.when(x < 2)
     def _():
-        for source in range(1, NY):
-            @pl.when(source <= y)
-            def _():
-                reduce_to_peers(source)
-
-    def to_owner(source):
-        owner_z = 8 * c + 2 * x + zs // 4
-        local = jnp.logical_and(jnp.logical_and(source == x, owner_z == z), zc == c)
-        slot = owned.at[lax.rem(zs, 4)]
-
-        @pl.when(jnp.logical_not(local))
-        def _():
-            send(total.at[source], slot, own_s.at[source], own_r, (source, owner_z, y, zc))
-
-        @pl.when(local)
-        def _():
-            pltpu.make_async_copy(total.at[source], slot, own_r).start()
-
-    def owner_sent(source):
-        owner_z = 8 * c + 2 * x + zs // 4
-        local = jnp.logical_and(jnp.logical_and(source == x, owner_z == z), zc == c)
-
-        @pl.when(jnp.logical_not(local))
-        def _():
-            wait(total.at[source], own_s.at[source])
-
-    to_owner(0)
+        for k in (2, 3):
+            taken_in(k)
+            pl.when(active(k))(lambda: reduce_to_peers(k))
+
+    pl.when(panel)(lambda: to_owner(0))
+    pl.when(jnp.logical_not(panel))(lambda: reduced(0))
 
     col_half = z // 8
     col_lanes = pl.ds(pl.multiple_of(lax.rem(z, 8) // 4 * 128, 128), 128)
@@ -241,6 +338,8 @@
         for half in range(NC):
             spread(tall.at[half], rows.at[x], rows_s.at[half], rows_r, NX, place_rows(half))
 
+    for k in range(1, NY):
+        reduced(k)
     wait(pivot, piv_r)
     wait(ty, ty_r)
     damp = jnp.sum(jnp.sum(ty[...], axis=0), keepdims=True) * (SCALE * 0.01 / FULL)
@@ -255,12 +354,6 @@
     for g in range(PANEL // 8):
         square[g, 0] = groups[g][0]
         square[g, 1] = groups[g][1]
-    for source in range(1, NY):
-        @pl.when(source <= y)
-        def _():
-            wait(inbox.at[source], z_r.at[source])
-            total[source] = jnp.sum(inbox[source], axis=0)
-            to_owner(source)
     groups = [[square[g, 0], square[g, 1]] for g in range(PANEL // 8)]
     eliminate(groups, PANEL // 2, PANEL, sub)
     scaled = []
@@ -287,7 +380,7 @@
     col_ids = strip0 + lax.broadcasted_iota(jnp.int32, (32, BLOCK), 0)
     row_ids = row0 + lax.broadcasted_iota(jnp.int32, (32, BLOCK), 1)
 
-    @pl.when(x <= y)
+    @pl.when(NC * x + z // 8 <= NC * y + c)
     def _():
         wait(owned, own_r)
     schur = owned[...].reshape(32, BLOCK) * SCALE + jnp.where(col_ids == row_ids, damp, 0.0) - wide
@@ -302,13 +395,13 @@
             @pl.when(target > y)
             def _():
                 wait(slices.at[y, piece], sl_s.at[target, piece])
-    owner_sent(0)
-    wait(partial.at[0, pl.ds(0, NZ - 1)], z_s.at[0])
-    for source in range(1, NY):
-        @pl.when(source <= y)
-        def _():
-            wait(partial.at[source, pl.ds(0, NZ - 1)], z_s.at[source])
-            owner_sent(source)
+    for k in range(NY):
+        owner_sent(k)
+        sent_to_peers(k)
+    for k in moved:
+        @pl.when(moved[k])
+        def _():
+            wait(partial.at[k], move_s.at[k])
     wait(tz.at[pl.ds(0, NZ - 1)], tz_s)
     wait(ty.at[pl.ds(0, NY - 1)], ty_s)
 
@@ -360,6 +453,7 @@
             dma((8,)), dma(()),
             dma((32,)), dma(()),
             dma((NY,)), dma(()),
+            dma((NY,)), dma((NY,)),
         ],
         compiler_params=pltpu.CompilerParams(collective_id=0, has_side_effects=True),
     )(a)

time: 77.1 us -> 70.1 us (0.909)
  the two profiles are of different devices: /device:TPU:26 before, /device:TPU:31 now
where the time goes in v3:
time: 70.1 us; the launch traced here: 69.9 us
  Pallas kernels  68.5 us (98%)
  local copies, waits for them, and re-layouts  1.38 us (2%)
    pallas_call x1, Pallas kernels, gathered(): pl.pallas_call(exchange, out_shape=jax.ShapeDtypeStruct((32, BLOCK), F32)...  68.5 us

profile of v3, /device:TPU:31, one launch (start us, length us, event | category | flops | bytes accessed | tf_op | source)
XLA Modules:
  0.0 69.9 jit_solution(12470711371030074808)
XLA Ops:
  0.0 68.5 %shard_map.17 = f32[32,256]{1,0:T(8,128)} custom-call(bf16[256,256]{1,0:T(8,128)(2,1)} %a_ref.1), custom_call_target="tpu_custom_call" | custom-call | tf_op jit(solution)/shard_map/pallas_call | solution.py:424
  68.5 1.4 %copy.3 = f32[256,32]{0,1:T(8,128)} copy(f32[256,32]{0,1:T(8,128)} %bitcast.1) | data formatting | bytes 65536

commit v4 on v3

--- a/solution.py
+++ b/solution.py
@@ -16,6 +16,10 @@
 FULL = BLOCK * NY * NC
 TOKENS = BLOCK * NX * NZ
 SCALE = 2.0 / TOKENS
+
+
+def far_first(i):
+    return NZ // 2 + jnp.where(lax.rem(i, 2) == 0, i // 2, -((i + 1) // 2))
 
 
 def wait(ref, sem):
@@ -78,9 +82,9 @@
 
 
 def exchange(a_ref, out_ref, feats, slices, partial, inbox, total, tall,
-             rows, cols, pivot, owned, tz, ty, tq, tr, square,
+             rows, cols, pivot, owned, tz, ty, tq, tr, square, hubs, strip, many,
              g1_s, g1_r, sib_s, sib_r, sl_s, sl_r, z_s, z_r, tz_s, tz_r, ty_s, ty_r, p1_s, p1_r,
-             rows_s, rows_r, cols_s, cols_r, piv_s, piv_r, own_s, own_r, move_s, move_r):
+             rows_s, rows_r, cols_s, cols_r, piv_s, piv_r, own_s, own_r, move_s, move_r, hub_s, hub_r):
     x, z, y, c = (lax.axis_index(name) for name in ("x", "z", "y", "c"))
     other = 1 - c
     mine = pl.ds(pl.multiple_of(x * SLICE, SLICE), SLICE)
@@ -144,9 +148,9 @@
     def reduce_to_peers(k):
         @pl.when(jnp.logical_not(halved(k)))
         def _():
-            @pl.loop(1, NZ)
+            @pl.loop(0, NZ - 1)
             def _(d):
-                target = lax.rem(z + d, NZ)
+                target = lax.rem(z + far_first(d), NZ)
                 send(partial.at[k, target], inbox.at[k, z], z_s.at[k], z_r.at[k], (x, target, y, c))
             pltpu.make_async_copy(partial.at[k, z], inbox.at[k, z], z_r.at[k]).start()
 
@@ -229,19 +233,23 @@
     arrived(0)
     multiply(0)
     reduce_to_peers(0)
-    acc = jnp.zeros((8, 128), F32)
-    for half in range(NC):
-        for piece in range(NX):
-            v = feats[half, piece].astype(F32)
-            v = jnp.sum((v * v).reshape(BLOCK // 8, 8, BLOCK), axis=0)
-            acc += v[:, :128] + v[:, 128:]
-    tq[...] = acc
-
-    @pl.loop(1, NZ)
-    def _(d):
-        target = lax.rem(z + d, NZ)
-        send(tq, tz.at[z], tz_s, tz_r, (x, target, y, c))
-    pltpu.make_async_copy(tq, tz.at[z], tz_r).start()
+    tracer = jnp.logical_and(x == NX - 1, c == 1)
+
+    @pl.when(tracer)
+    def _():
+        acc = jnp.zeros((8, 128), F32)
+        for half in range(NC):
+            for piece in range(NX):
+                v = feats[half, piece].astype(F32)
+                v = jnp.sum((v * v).reshape(BLOCK // 8, 8, BLOCK), axis=0)
+                acc += v[:, :128] + v[:, 128:]
+        tq[...] = acc
+
+        @pl.loop(0, NZ - 1)
+        def _(d):
+            target = lax.rem(z + far_first(d), NZ)
+            send(tq, tz.at[z], tz_s, tz_r, (x, target, y, c))
+        pltpu.make_async_copy(tq, tz.at[z], tz_r).start()
 
     for k in (2, 3, 1):
         @pl.when(k <= y)
@@ -252,7 +260,7 @@
             @pl.when(moved[k])
             def _():
                 send(partial.at[k], partial.at[k], move_s.at[k], move_r.at[k], (x, z, NY - 1 - y, c))
-    pl.when(active(1))(lambda: reduce_to_peers(1))
+    pl.when(jnp.logical_and(active(1), jnp.logical_not(panel)))(lambda: reduce_to_peers(1))
 
     @pl.when(x >= 2)
     def _():
@@ -260,24 +268,37 @@
             taken_in(k)
             pl.when(active(k))(lambda: reduce_to_peers(k))
 
+    pl.when(jnp.logical_not(panel))(lambda: reduced(0))
+    piv_chunk = total.at[0, :, pl.ds(0, 128)]
+    hub = jnp.logical_and(y == 0, c == 0)
+
     @pl.when(panel)
     def _():
         wait(inbox.at[0], z_r.at[0])
         total[0] = jnp.sum(inbox[0], axis=0)
 
-        @pl.loop(1, NZ)
+        @pl.when(jnp.logical_and(y == 0, zc == 0))
+        def _():
+            @pl.loop(0, NX * NZ)
+            def _(i):
+                tx = lax.rem(x + i // NZ, NX)
+                tz_ = lax.rem(z + NZ // 2 + i, NZ)
+                here = jnp.logical_and(tx == x, tz_ == z)
+
+                @pl.when(here)
+                def _():
+                    pltpu.make_async_copy(piv_chunk, hubs.at[x, zs], hub_r).start()
+
+                @pl.when(jnp.logical_not(here))
+                def _():
+                    send(piv_chunk, hubs.at[x, zs], hub_s, hub_r, (tx, tz_, y, c))
+
+        @pl.loop(0, NZ - 1)
         def _(d):
-            target = lax.rem(z + d, NZ)
+            target = lax.rem(z + far_first(d), NZ)
             send(total.at[0], tall.at[zc, zs], p1_s, p1_r, (x, target, y, c))
         pltpu.make_async_copy(total.at[0], tall.at[zc, zs], p1_r).start()
-
-    wait(tz, tz_r)
-    tr[...] = jnp.sum(tz[...], axis=0)
-
-    @pl.loop(1, NY)
-    def _(d):
-        send(tr, ty.at[y], ty_s, ty_r, (x, z, lax.rem(y + d, NY), c))
-    pltpu.make_async_copy(tr, ty.at[y], ty_r).start()
+        pl.when(active(1))(lambda: reduce_to_peers(1))
 
     @pl.when(x < 2)
     def _():
@@ -286,10 +307,26 @@
             pl.when(active(k))(lambda: reduce_to_peers(k))
 
     pl.when(panel)(lambda: to_owner(0))
-    pl.when(jnp.logical_not(panel))(lambda: reduced(0))
-
-    col_half = z // 8
-    col_lanes = pl.ds(pl.multiple_of(lax.rem(z, 8) // 4 * 128, 128), 128)
+
+    @pl.when(tracer)
+    def _():
+        wait(tz, tz_r)
+        tr[...] = jnp.sum(tz[...], axis=0)
+
+        @pl.loop(1, NX * NY * NC)
+        def _(i):
+            there = (lax.rem(x + i // (NY * NC), NX), z, lax.rem(y + i // NC, NY), lax.rem(c + i, NC))
+            send(tr, ty.at[y], ty_s, ty_r, there)
+        pltpu.make_async_copy(tr, ty.at[y], ty_r).start()
+
+    @pl.when(hub)
+    def _():
+        wait(hubs, hub_r)
+
+        @pl.loop(1, NY * NC)
+        def _(i):
+            send(hubs, pivot, piv_s.at[i], piv_r, (x, z, lax.rem(y + i // NC, NY), lax.rem(c + i, NC)))
+        pltpu.make_async_copy(hubs, pivot, piv_r).start()
 
     def spread(src, dst, sems, recv, count, place):
         @pl.loop(0, count)
@@ -315,31 +352,27 @@
             def _():
                 wait(src, sems.at[i])
 
-    def place_pivot(i):
-        return i // 8, lax.rem(i // 2, NY), lax.rem(i, NC)
-
     def place_cols(i):
         return y, i // 2, lax.rem(i, NC)
 
     def place_rows(half):
         return lambda i: (i, y, half)
 
-    pivot_src = tall.at[0, :, :, pl.ds(0, 128)]
-    cols_src = tall.at[col_half, :, :, col_lanes]
-
     @pl.when(panel)
     def _():
         wait(tall, p1_r)
-
-        @pl.when(y == 0)
-        def _():
-            spread(pivot_src, pivot.at[x], piv_s, piv_r, 32, place_pivot)
-        spread(cols_src, cols.at[x], cols_s, cols_r, 8, place_cols)
+        mixed = tall[z // 8].reshape(SLICE, BLOCK)
+        mixed = jnp.where(lax.rem(z, 8) >= 4, mixed[:, 128:], mixed[:, :128])
+        lanes = lax.broadcasted_iota(jnp.int32, (16, 128), 1) // 32
+        packed = jnp.zeros((16, 128), F32)
+        for q in range(4):
+            turned = pltpu.roll(mixed[16 * q:16 * q + 16], lax.rem(32 * q - 32 * lax.rem(z, 4) + 128, 128), 1)
+            packed = jnp.where(lanes == q, turned, packed)
+        strip[...] = packed
         for half in range(NC):
             spread(tall.at[half], rows.at[x], rows_s.at[half], rows_r, NX, place_rows(half))
-
-    for k in range(1, NY):
-        reduced(k)
+        spread(strip, cols.at[x], cols_s, cols_r, 8, place_cols)
+
     wait(pivot, piv_r)
     wait(ty, ty_r)
     damp = jnp.sum(jnp.sum(ty[...], axis=0), keepdims=True) * (SCALE * 0.01 / FULL)
@@ -354,6 +387,8 @@
     for g in range(PANEL // 8):
         square[g, 0] = groups[g][0]
         square[g, 1] = groups[g][1]
+    for k in range(1, NY):
+        reduced(k)
     groups = [[square[g, 0], square[g, 1]] for g in range(PANEL // 8)]
     eliminate(groups, PANEL // 2, PANEL, sub)
     scaled = []
@@ -369,14 +404,14 @@
     right = rows[...].reshape(PANEL, BLOCK) * SCALE + jnp.where(ids == row_ids, damp, 0.0)
     highest = lax.Precision.HIGHEST
     right = jnp.dot(inverse, right, precision=highest, preferred_element_type=F32)
-    left = jnp.dot(inverse, cols[...].reshape(PANEL, PANEL) * SCALE, precision=highest, preferred_element_type=F32)
+    left = jnp.concatenate([pltpu.roll(cols[h], (128 - 32 * q) % 128, 1) for h in range(2) for q in range(4)], axis=0)
+    left = jnp.dot(inverse, left * SCALE, precision=highest, preferred_element_type=F32)
     update = lax.dot_general(left, right, (((0,), (0,)), ((), ())), precision=highest, preferred_element_type=F32)
     strip0 = (x * NZ + z) * 32
     leading = strip0 < PANEL
-    picked = jnp.where(leading, right, update)
-    wide = jnp.zeros((32, BLOCK), F32)
+    wide = update[:32]
     for q in range(4):
-        wide = jnp.where(lax.rem(z, 4) == q, picked[32 * q:32 * q + 32], wide)
+        wide = jnp.where(jnp.logical_and(leading, z == q), right[32 * q:32 * q + 32], wide)
     col_ids = strip0 + lax.broadcasted_iota(jnp.int32, (32, BLOCK), 0)
     row_ids = row0 + lax.broadcasted_iota(jnp.int32, (32, BLOCK), 1)
 
@@ -402,18 +437,25 @@
         @pl.when(moved[k])
         def _():
             wait(partial.at[k], move_s.at[k])
-    wait(tz.at[pl.ds(0, NZ - 1)], tz_s)
-    wait(ty.at[pl.ds(0, NY - 1)], ty_s)
+    @pl.when(tracer)
+    def _():
+        wait(tz.at[pl.ds(0, NZ - 1)], tz_s)
+        wait(many.at[pl.ds(0, NX * NY * NC - 1)], ty_s)
+
+    @pl.when(hub)
+    def _():
+        @pl.loop(1, NY * NC)
+        def _(i):
+            wait(hubs, piv_s.at[i])
 
     @pl.when(panel)
     def _():
-        for _ in range(1):
-            wait(inbox.at[0, pl.ds(0, NZ - 1)], p1_s)
-
-        @pl.when(y == 0)
-        def _():
-            spread_done(pivot_src, piv_s, 32, place_pivot)
-        spread_done(cols_src, cols_s, 8, place_cols)
+        wait(inbox.at[0, pl.ds(0, NZ - 1)], p1_s)
+
+        @pl.when(jnp.logical_and(y == 0, zc == 0))
+        def _():
+            wait(many.at[pl.ds(0, NX * NZ - 1)], hub_s)
+        spread_done(strip, cols_s, 8, place_cols)
         for half in range(NC):
             spread_done(tall.at[half], rows_s.at[half], NX, place_rows(half))
 
@@ -434,7 +476,7 @@
             pltpu.VMEM((NY, 8, BLOCK), F32),
             pltpu.VMEM((NC, 8, 8, BLOCK), F32),
             pltpu.VMEM((2, 8, 8, BLOCK), F32),
-            pltpu.VMEM((2, 8, 8, 128), F32),
+            pltpu.VMEM((2, 16, 128), F32),
             pltpu.VMEM((2, 8, 8, 128), F32),
             pltpu.VMEM((4, 8, BLOCK), F32),
             pltpu.VMEM((NZ, 8, 128), F32),
@@ -442,6 +484,9 @@
             pltpu.VMEM((8, 128), F32),
             pltpu.VMEM((8, 128), F32),
             pltpu.VMEM((PANEL // 8, 2, 8, PANEL), F32),
+            pltpu.VMEM((2, 8, 8, 128), F32),
+            pltpu.VMEM((16, 128), F32),
+            pltpu.VMEM((64, 8, 128), F32),
             dma((NX,)), dma((NX,)),
             dma((NX,)), dma((NX,)),
             dma((NY, NX)), dma((NY, NX)),
@@ -451,9 +496,10 @@
             dma(()), dma(()),
             dma((NC, NX)), dma(()),
             dma((8,)), dma(()),
-            dma((32,)), dma(()),
+            dma((8,)), dma(()),
             dma((NY,)), dma(()),
             dma((NY,)), dma((NY,)),
+            dma(()), dma(()),
         ],
         compiler_params=pltpu.CompilerParams(collective_id=0, has_side_effects=True),
     )(a)

time: 70.1 us -> 62.5 us (0.89)
  the two profiles are of different devices: /device:TPU:31 before, /device:TPU:51 now
where the time goes in v4:
time: 62.5 us; the launch traced here: 62.3 us
  Pallas kernels  60.9 us (97%)
  local copies, waits for them, and re-layouts  1.38 us (2%)
    pallas_call x1, Pallas kernels, gathered(): pl.pallas_call(exchange, out_shape=jax.ShapeDtypeStruct((32, BLOCK), F32)...  60.9 us
    unnamed x1, local copies, waits for them, and re-layouts  1.38 us

profile of v4, /device:TPU:51, one launch (start us, length us, event | category | flops | bytes accessed | tf_op | source)
XLA Modules:
  0.0 62.3 jit_solution(8624760898685833561)
XLA Ops:
  0.0 60.9 %shard_map.17 = f32[32,256]{1,0:T(8,128)} custom-call(bf16[256,256]{1,0:T(8,128)(2,1)} %a_ref.1), custom_call_target="tpu_custom_call" | custom-call | tf_op jit(solution)/shard_map/pallas_call | solution.py:466
  60.9 1.4 %copy.3 = f32[256,32]{0,1:T(8,128)} copy(f32[256,32]{0,1:T(8,128)} %bitcast.1) | data formatting | bytes 65536

commit v5 on v4

v5 whole, which is shorter than its diff:
```python
import jax
import jax.numpy as jnp
from jax import lax
from jax.experimental import pallas as pl
from jax.experimental.pallas import tpu as pltpu
from jax.sharding import Mesh
from jax.sharding import PartitionSpec as P

MESH = pl.DeviceIdType.MESH
F32 = jnp.float32
BF16 = jnp.bfloat16
NX, NZ, NY, NC = 4, 16, 4, 2
BLOCK = 256
PANEL = 128
SLICE = BLOCK // NX
STRIPS = 8
FULL = BLOCK * NY * NC
TOKENS = BLOCK * NX * NZ
SCALE = 2.0 / TOKENS
PLANE = NX * NY * NC
GATES = 1


def wait(ref, sem):
    pltpu.make_async_copy(ref, ref, sem).wait()


def local(src, dst, sem):
    pltpu.make_async_copy(src, dst, sem).start()


def send(src, dst, send_sem, recv_sem, device):
    pltpu.make_async_remote_copy(
        src_ref=src,
        dst_ref=dst,
        send_sem=send_sem,
        recv_sem=recv_sem,
        device_id=device,
        device_id_type=MESH,
    ).start()


def far_first(i):
    return NZ // 2 + jnp.where(lax.rem(i, 2) == 0, i // 2, -((i + 1) // 2))


def both(*conditions):
    out = conditions[0]
    for condition in conditions[1:]:
        out = jnp.logical_and(out, condition)
    return out


def neither(condition):
    return jnp.logical_not(condition)


def spread_rows(row):
    return jnp.broadcast_to(row, (8, PANEL))


def spread_lane(tile, lane):
    return jnp.broadcast_to(tile[:, lane:lane + 1], (8, PANEL))


def eliminate(groups, first, last, sub):
    for k in range(first, last, 4):
        g0, r0 = k // 8, k % 8
        head = groups[g0]
        rows = [[spread_rows(head[h][r0 + i:r0 + i + 1]) for h in range(2)] for i in range(4)]
        dots = [[spread_lane(rows[i][0], k + j) if j >= i else None for j in range(4)] for i in range(4)]
        mults = [[None] * 4 for _ in range(4)]
        scaled = []
        for i in range(4):
            inv = 1.0 / dots[i][i]
            for j in range(i + 1, 4):
                mults[i][j] = dots[i][j] * inv
            for j in range(i + 1, 4):
                for l in range(j, 4):
                    dots[j][l] = dots[j][l] - mults[i][j] * dots[i][l]
                rows[j] = [rows[j][h] - mults[i][j] * rows[i][h] for h in range(2)]
            scaled.append([rows[i][h] * inv for h in range(2)])
        for i in (2, 1, 0):
            for j in range(i + 1, 4):
                scaled[i] = [scaled[i][h] - mults[i][j] * scaled[j][h] for h in range(2)]
        for g in range(g0 if r0 == 0 else g0 + 1, PANEL // 8):
            tile = groups[g]
            new = list(tile)
            for j in range(4):
                factor = spread_lane(tile[0], k + j)
                new = [new[h] - factor * scaled[j][h] for h in range(2)]
            if g == g0:
                new = [jnp.where(sub > 3, new[h], tile[h]) for h in range(2)]
            groups[g] = new
        for h in range(2):
            tile = groups[g0][h]
            for i in range(4):
                tile = jnp.where(sub == r0 + i, rows[i][h], tile)
            groups[g0] = [tile, groups[g0][1]] if h == 0 else [groups[g0][0], tile]


def exchange(a_ref, out_ref, feats, slices, partial, inbox, total, pin, psum, tall, rows, cols, pivot, owned,
             tz, ty, tq, tr, square, hubs, strip, many, gram, gin, gpart, gx, gtot,
             g1_s, g1_r, sib_s, sib_r, sl_s, sl_r, z_s, z_r, tz_s, tz_r, ty_s, ty_r, p0_s, p0_r, p1_s, p1_r,
             rows_s, rows_r, cols_s, cols_r, piv_s, piv_r, own_s, own_r, move_s, move_r, hub_s, hub_r, gz_s, gz_r, gx_s, gx_r, gate):
    x, z, y, c = (lax.axis_index(name) for name in ("x", "z", "y", "c"))
    other = 1 - c

    def along(d):
        return (x, lax.rem(z + d + NZ, NZ), y, c)

    def in_plane(i):
        return (lax.rem(x + i // (NY * NC), NX), z, lax.rem(y + i // NC, NY), lax.rem(c + i, NC))

    barrier = pltpu.get_barrier_semaphore()

    @pl.loop(1, PLANE)
    def _(i):
        pl.semaphore_signal(barrier, inc=1, device_id=in_plane(i), device_id_type=MESH)

    @pl.loop(1, NZ)
    def _(d):
        pl.semaphore_signal(barrier, inc=1, device_id=along(d), device_id_type=MESH)

    feats[c, x] = a_ref[...].T
    pl.semaphore_wait(barrier, PLANE - 1 + NZ - 1)
    hub = both(y == 0, c == 0)
    panel = c == 0
    place = lax.rem(z + 4, NZ)
    holder = both(panel, place < STRIPS)
    place_s, place_h = place // NC, lax.rem(place, NC)

    def part(piece, h):
        return feats.at[c, piece, pl.ds(128 * h, 128)]

    def pass_on(piece, h, step, sem):
        send(part(piece, h), part(piece, h), g1_s.at[sem], g1_r.at[piece, h], (lax.rem(x + step, NX), z, y, c))

    def relay(piece, h):
        send(part(piece, h), part(piece, h), sib_s.at[piece], sib_r.at[piece], (x, z, y, other))
        parts = []
        for k in range(4 * h, 4 * h + 4):
            start = pl.multiple_of(32 * k + 16 * (x // 2), 16)
            tile = feats[c, piece, pl.ds(start, 16)].astype(F32)
            parts.append(jnp.where(lax.rem(x, 2) == 1, tile[8:], tile[:8]))
        slices[y, piece, pl.ds(32 * h, 32)] = jnp.concatenate(parts, axis=0).astype(BF16)
        for target in range(1, NY):
            @pl.when(target > y)
            def _():
                there = slices.at[y, piece, pl.ds(32 * h, 32)]
                send(there, there, sl_s.at[target, piece], sl_r.at[y, piece], (x, z, target, c))

    pass_on(x, 0, 1, 0)
    pass_on(x, 1, 3, 1)
    pass_on(x, 1, 1, 2)
    pass_on(x, 0, 3, 3)
    relay(x, 0)
    relay(x, 1)

    def gram_out():
        block = feats[c, x, :PANEL]
        block = lax.dot_general(block, block, (((1,), (1,)), ((), ())), preferred_element_type=F32)
        gram[...] = block.reshape(STRIPS, 16, PANEL)
        for n in range(STRIPS):
            target = (12 + n) % NZ
            pl.when(target == z)(lambda: local(gram.at[n], gin.at[z], gz_r))
            pl.when(target != z)(lambda: send(gram.at[n], gin.at[z], gz_s, gz_r, (x, target, y, c)))

    left_x, right_x, far_x = lax.rem(x + 3, NX), lax.rem(x + 1, NX), lax.rem(x + 2, NX)
    for i, (piece, h, step) in enumerate(
        ((left_x, 0, 1), (right_x, 1, 3), (left_x, 1, 0), (right_x, 0, 0), (far_x, 0, 0), (far_x, 1, 0))
    ):
        wait(part(piece, h), g1_r.at[piece, h])
        if step:
            pass_on(piece, h, step, 4 + h)
        relay(piece, h)
        if i == 0:
            pl.when(hub)(gram_out)

    @pl.when(both(hub, holder))
    def _():
        wait(gin, gz_r)
        gpart[...] = jnp.sum(gin[...], axis=0)
        for d in (1, 3, 2):
            send(gpart, gx.at[x], gx_s.at[d], gx_r, (lax.rem(x + d, NX), z, y, c))
        local(gpart, gx.at[x], gx_r)
    for piece in range(NX):
        wait(feats.at[other, piece], sib_r.at[piece])

    moved = {2: y == 3}
    taken = {2: y == 0}
    gets = z // STRIPS == c

    def owner_row(k):
        return jnp.where(taken[k], NY - 1 - y, y) if k in taken else y

    def active(k):
        own = k <= y
        return jnp.logical_or(both(own, neither(moved[k])), taken[k]) if k in moved else own

    def halved(k):
        return both(c == 1, y == k)

    def first_strip(k):
        return jnp.where(panel, 4, 0) if k == 0 else 0

    def receives(k):
        return both(gets, active(k), lax.rem(z, STRIPS) >= first_strip(k))

    def arrived(source):
        @pl.when(source < y)
        def _():
            for piece in range(NX):
                wait(slices.at[source, piece], sl_r.at[source, piece])

    def multiply(source):
        for half in range(NC):
            acc = jnp.zeros((SLICE, BLOCK), F32)
            for piece in range(NX):
                acc += lax.dot_general(slices[source, piece], feats[half, piece], (((1,), (1,)), ((), ())),
                                       preferred_element_type=F32)
            for s in range(STRIPS):
                partial[source, s, half] = acc[8 * s:8 * s + 8]

    def reduce_to_peers(ks, when):
        @pl.loop(0, NZ)
        def _(i):
            target = lax.rem(z + jnp.where(i == NZ - 1, 0, far_first(i)), NZ)
            s = lax.rem(target, STRIPS)
            for k in ks:
                src, dst = partial.at[k, s], inbox.at[k, z]
                fits = both(when(k), target // STRIPS == c, s >= first_strip(k))

                def go(src, dst):
                    pl.when(target == z)(lambda: local(src, dst, z_r.at[k]))
                    pl.when(target != z)(lambda: send(src, dst, z_s.at[k], z_r.at[k], (x, target, y, c)))

                pl.when(both(fits, neither(halved(k))))(lambda: go(src, dst))
                pl.when(both(fits, halved(k)))(lambda: go(src.at[1], dst.at[1]))

    def sent_to_peers(k):
        count = STRIPS - first_strip(k) - jnp.where(receives(k), 1, 0)
        for n in (3, 4, 7, 8):
            if n < 5 and k > 0:
                continue

            @pl.when(both(active(k), count == n, neither(halved(k))))
            def _():
                wait(partial.at[k, pl.ds(0, n)], z_s.at[k])

            @pl.when(both(active(k), count == n, halved(k)))
            def _():
                wait(partial.at[k, pl.ds(0, n), 1], z_s.at[k])

    def owners(k, act):
        for half in range(NC):
            needed = receives(k) if half == 1 else both(receives(k), neither(halved(k)))
            here = both(k == x, owner_row(k) == y, half == c)

            if act == "start":
                pl.when(both(needed, here))(lambda: local(total.at[k, half], owned.at[x], own_r))

            @pl.when(both(needed, neither(here)))
            def _():
                if act == "start":
                    send(total.at[k, half], owned.at[x], own_s.at[k, half], own_r, (k, z, owner_row(k), half))
                else:
                    wait(total.at[k, half], own_s.at[k, half])

    def reduced(k):
        @pl.when(both(receives(k), neither(halved(k))))
        def _():
            wait(inbox.at[k], z_r.at[k])
            total[k] = jnp.sum(inbox[k], axis=0)

        @pl.when(both(receives(k), halved(k)))
        def _():
            wait(inbox.at[k, :, 1], z_r.at[k])
            total[k, 1] = jnp.sum(inbox[k, :, 1], axis=0)
        owners(k, "start")

    def taken_in(k):
        if k in taken:
            @pl.when(taken[k])
            def _():
                wait(partial.at[k], move_r.at[k])

    arrived(0)
    multiply(0)

    @pl.when(panel)
    def _():
        for n in range(STRIPS):
            target = (12 + n) % NZ

            @pl.when(target == z)
            def _():
                local(partial.at[0, n // NC, n % NC], pin.at[z], p0_r)

            @pl.when(target != z)
            def _():
                send(partial.at[0, n // NC, n % NC], pin.at[z], p0_s, p0_r, (x, target, y, c))

    @pl.when(both(hub, holder))
    def _():
        wait(gx, gx_r)
        gtot[...] = jnp.sum(gx[...], axis=0)

        @pl.loop(0, NZ - 1)
        def _(d):
            send(gtot, hubs.at[place], hub_s, hub_r, along(far_first(d)))
        local(gtot, hubs.at[place], hub_r)

    tracer = both(x == NX - 1, c == 1)

    @pl.when(tracer)
    def _():
        acc = jnp.zeros((8, 128), F32)
        for half in range(NC):
            for piece in range(NX):
                v = feats[half, piece].astype(F32)
                v = jnp.sum((v * v).reshape(BLOCK // 8, 8, BLOCK), axis=0)
                acc += v[:, :128] + v[:, 128:]
        tq[...] = acc

        @pl.loop(0, NZ - 1)
        def _(d):
            send(tq, tz.at[z], tz_s, tz_r, along(far_first(d)))
        local(tq, tz.at[z], tz_r)

    for k in (2, 3, 1):
        @pl.when(k <= y)
        def _():
            arrived(k)
            multiply(k)
        if k in moved:
            @pl.when(moved[k])
            def _():
                send(partial.at[k], partial.at[k], move_s.at[k], move_r.at[k], (x, z, NY - 1 - y, c))

    def kept(k):
        return both(active(k), neither(taken[k])) if k in taken else active(k)

    pl.when(panel)(lambda: reduce_to_peers((0, 1), kept))

    @pl.when(holder)
    def _():
        wait(pin, p0_r)
        psum[...] = jnp.sum(pin[...], axis=0)

        @pl.loop(0, NZ - 1)
        def _(d):
            send(psum, tall.at[place_h, place_s], p1_s, p1_r, along(far_first(d)))
        local(psum, tall.at[place_h, place_s], p1_r)

    pl.when(panel)(lambda: reduce_to_peers((2, 3), kept))

    @pl.when(neither(panel))
    def _():
        for n in range(GATES):
            pl.semaphore_signal(gate.at[n], inc=1, device_id=along(8), device_id_type=MESH)
            pl.semaphore_wait(gate.at[n], 1)
        reduce_to_peers((0, 1, 2, 3), kept)

    taken_in(2)
    pl.when(taken[2])(lambda: reduce_to_peers((2,), active))

    @pl.when(tracer)
    def _():
        wait(tz, tz_r)
        tr[...] = jnp.sum(tz[...], axis=0)

        @pl.loop(1, PLANE)
        def _(i):
            send(tr, ty.at[y], ty_s, ty_r, in_plane(i))
        local(tr, ty.at[y], ty_r)

    @pl.when(hub)
    def _():
        wait(hubs, hub_r)

        @pl.loop(1, NY * NC)
        def _(i):
            send(hubs, pivot, piv_s.at[i], piv_r, (x, z, lax.rem(y + i // NC, NY), lax.rem(c + i, NC)))
        local(hubs, pivot, piv_r)

    def spread(src, dst, sems, recv, count, where, start):
        @pl.loop(0, count)
        def _(i):
            tx, to_y, tc = where(i)
            here = both(tx == x, to_y == y, tc == c)
            if start:
                pl.when(here)(lambda: local(src, dst, recv))
                pl.when(neither(here))(lambda: send(src, dst, sems.at[i], recv, (tx, z, to_y, tc)))
            else:
                pl.when(neither(here))(lambda: wait(src, sems.at[i]))

    def spread_panel(start):
        for half in range(NC):
            spread(tall.at[half], rows.at[x], rows_s.at[half], rows_r, NX, lambda i: (lax.rem(x + i, NX), y, half), start)
        spread(strip, cols.at[x], cols_s, cols_r, NY * NC, lambda i: (y, i // 2, lax.rem(i, NC)), start)

    @pl.when(panel)
    def _():
        wait(tall, p1_r)
        mixed = tall[z // 8].reshape(32, BLOCK)
        mixed = jnp.where(lax.rem(z, 8) >= 4, mixed[:, 128:], mixed[:, :128])
        lanes = lax.broadcasted_iota(jnp.int32, (8, 128), 1) // 32
        packed = jnp.zeros((8, 128), F32)
        for q in range(4):
            turned = pltpu.roll(mixed[8 * q:8 * q + 8], lax.rem(32 * q - 32 * lax.rem(z, 4) + 128, 128), 1)
            packed = jnp.where(lanes == q, turned, packed)
        strip[...] = packed
        spread_panel(True)

    wait(pivot, piv_r)
    wait(ty, ty_r)
    damp = jnp.sum(jnp.sum(ty[...], axis=0), keepdims=True) * (SCALE * 0.01 / FULL)
    lane = lax.broadcasted_iota(jnp.int32, (8, PANEL), 1)
    sub = lax.broadcasted_iota(jnp.int32, (8, PANEL), 0)
    groups = []
    for g in range(PANEL // 8):
        diag = lane == sub + 8 * g
        left = pivot[g // 2, 8 * (g % 2):8 * (g % 2) + 8] * SCALE + jnp.where(diag, damp, 0.0)
        groups.append([left, jnp.where(diag, 1.0, 0.0).astype(F32)])
    eliminate(groups, 0, PANEL // 2, sub)
    for g in range(PANEL // 8):
        square[g, 0] = groups[g][0]
        square[g, 1] = groups[g][1]
    for k in range(NY):
        reduced(k)
    groups = [[square[g, 0], square[g, 1]] for g in range(PANEL // 8)]
    eliminate(groups, PANEL // 2, PANEL, sub)
    scaled = []
    for g in range(PANEL // 8):
        diag = jnp.sum(jnp.where(lane == sub + 8 * g, groups[g][0], 0.0), axis=1, keepdims=True)
        scaled.append(groups[g][1] * lax.rsqrt(diag))
    inverse = jnp.concatenate(scaled, axis=0)
    wait(cols, cols_r)
    wait(rows, rows_r)
    ids = lax.broadcasted_iota(jnp.int32, (PANEL, BLOCK), 0)
    row0 = (y * NC + c) * BLOCK
    row_ids = row0 + lax.broadcasted_iota(jnp.int32, (PANEL, BLOCK), 1)
    right = jnp.concatenate([rows[i, q] for q in range(4) for i in range(NX)], axis=0)
    right = right * SCALE + jnp.where(ids == row_ids, damp, 0.0)
    highest = lax.Precision.HIGHEST
    right = jnp.dot(inverse, right, precision=highest, preferred_element_type=F32)
    left = jnp.concatenate([pltpu.roll(cols[i], (128 - 32 * q) % 128, 1) for q in range(4) for i in range(NX)], axis=0)
    left = jnp.dot(inverse, left * SCALE, precision=highest, preferred_element_type=F32)
    update = lax.dot_general(left, right, (((0,), (0,)), ((), ())), precision=highest, preferred_element_type=F32)
    strip0 = (x * NZ + z) * 32
    leading = strip0 < PANEL
    wide = update[:32]
    for q in range(4):
        wide = jnp.where(both(leading, z == q), right[32 * q:32 * q + 32], wide)
    col_ids = strip0 + lax.broadcasted_iota(jnp.int32, (32, BLOCK), 0)
    row_ids = row0 + lax.broadcasted_iota(jnp.int32, (32, BLOCK), 1)

    @pl.when(both(neither(leading), NC * x + z // 8 <= NC * y + c))
    def _():
        wait(owned, own_r)
    schur = owned[...].reshape(32, BLOCK) * SCALE + jnp.where(col_ids == row_ids, damp, 0.0) - wide
    wide = jnp.where(leading, wide, schur)
    out_ref[...] = jnp.where(row_ids >= col_ids, wide, 0.0)

    for h in range(2):
        for sem in (0, 1, 2, 3, 4, 5):
            if sem in (0, 3) and h == 0 or sem in (1, 2) and h == 1 or sem == 4 + h:
                wait(part(x, h), g1_s.at[sem])
    for piece in range(NX):
        wait(feats.at[c, piece], sib_s.at[piece])
        for target in range(1, NY):
            @pl.when(target > y)
            def _():
                wait(slices.at[y, piece], sl_s.at[target, piece])
    for k in range(NY):
        sent_to_peers(k)
        owners(k, "finish")
    for k in moved:
        @pl.when(moved[k])
        def _():
            wait(partial.at[k], move_s.at[k])

    @pl.when(tracer)
    def _():
        wait(tz.at[pl.ds(0, NZ - 1)], tz_s)
        wait(many.at[pl.ds(0, PLANE - 1)], ty_s)

    @pl.when(hub)
    def _():
        @pl.loop(1, NY * NC)
        def _(i):
            wait(hubs, piv_s.at[i])

    @pl.when(holder)
    def _():
        wait(pin.at[pl.ds(0, STRIPS - 1)], p0_s)
        wait(pin.at[pl.ds(0, NZ - 1)], p1_s)

    @pl.when(both(hub, holder))
    def _():
        wait(gram.at[pl.ds(0, STRIPS - 1)], gz_s)
        for d in (1, 3, 2):
            wait(gpart, gx_s.at[d])
        wait(gin.at[pl.ds(0, NZ - 1)], hub_s)

    @pl.when(both(hub, neither(holder)))
    def _():
        wait(gram, gz_s)

    @pl.when(both(panel, neither(holder)))
    def _():
        wait(pin.at[pl.ds(0, STRIPS)], p0_s)
    pl.when(panel)(lambda: spread_panel(False))


def shards(a):
    dma = pltpu.SemaphoreType.DMA
    vmem = pl.BlockSpec(memory_space=pltpu.VMEM)
    result = pl.pallas_call(
        exchange,
        out_shape=jax.ShapeDtypeStruct((32, BLOCK), F32),
        in_specs=[vmem],
        out_specs=vmem,
        scratch_shapes=[
            pltpu.VMEM((NC, NX, BLOCK, BLOCK), BF16),
            pltpu.VMEM((NY, NX, SLICE, BLOCK), BF16),
            pltpu.VMEM((NY, STRIPS, NC, 8, BLOCK), F32),
            pltpu.VMEM((NY, NZ, NC, 8, BLOCK), F32),
            pltpu.VMEM((NY, NC, 8, BLOCK), F32),
            pltpu.VMEM((NZ, 8, BLOCK), F32),
            pltpu.VMEM((8, BLOCK), F32),
            pltpu.VMEM((NC, 4, 8, BLOCK), F32),
            pltpu.VMEM((NX, 4, 8, BLOCK), F32),
            pltpu.VMEM((NX, 8, 128), F32),
            pltpu.VMEM((STRIPS, 16, 128), F32),
            pltpu.VMEM((NX, 8, BLOCK), F32),
            pltpu.VMEM((NZ, 8, 128), F32),
            pltpu.VMEM((NY, 8, 128), F32),
            pltpu.VMEM((8, 128), F32),
            pltpu.VMEM((8, 128), F32),
            pltpu.VMEM((PANEL // 8, 2, 8, PANEL), F32),
            pltpu.VMEM((STRIPS, 16, 128), F32),
            pltpu.VMEM((8, 128), F32),
            pltpu.VMEM((PLANE, 8, 128), F32),
            pltpu.VMEM((STRIPS, 16, 128), F32),
            pltpu.VMEM((NZ, 16, 128), F32),
            pltpu.VMEM((16, 128), F32),
            pltpu.VMEM((NX, 16, 128), F32),
            pltpu.VMEM((16, 128), F32),
            dma((6,)), dma((NX, 2)),
            dma((NX,)), dma((NX,)),
            dma((NY, NX)), dma((NY, NX)),
            dma((NY,)), dma((NY,)),
            dma(()), dma(()),
            dma(()), dma(()),
            dma(()), dma(()),
            dma(()), dma(()),
            dma((NC, NX)), dma(()),
            dma((NY * NC,)), dma(()),
            dma((NY * NC,)), dma(()),
            dma((NY, NC)), dma(()),
            dma((NY,)), dma((NY,)),
            dma(()), dma(()),
            dma(()), dma(()),
            dma((NX,)), dma(()),
            pltpu.SemaphoreType.REGULAR((2,)),
        ],
        compiler_params=pltpu.CompilerParams(collective_id=0, has_side_effects=True),
    )(a)
    return result.T


def solution(mesh):
    finer = Mesh(mesh.devices.reshape(NX, NZ, NY, NC), ("x", "z", "y", "c"))
    return jax.shard_map(
        shards, mesh=finer, in_specs=(P(("x", "z"), ("y", "c")),), out_specs=P(("y", "c"), ("x", "z")), check_vma=False
    )
```

time: 62.5 us -> 57.1 us (0.914)
  the two profiles are of different devices: /device:TPU:51 before, /device:TPU:120 now
where the time goes in v5:
time: 57.1 us; the launch traced here: 56.9 us
  Pallas kernels  55.6 us (97%)
  local copies, waits for them, and re-layouts  1.38 us (2%)
    pallas_call x1, Pallas kernels, shards(): pl.pallas_call(exchange, out_shape=jax.ShapeDtypeStruct((32, BLOCK), F32)...  55.6 us
    unnamed x1, local copies, waits for them, and re-layouts  1.38 us

profile of v5, /device:TPU:120, one launch (start us, length us, event | category | flops | bytes accessed | tf_op | source)
XLA Modules:
  0.0 56.9 jit_solution(16331787370547797339)
XLA Ops:
  0.0 55.6 %shard_map.17 = f32[32,256]{1,0:T(8,128)} custom-call(bf16[256,256]{1,0:T(8,128)(2,1)} %a_ref.1), custom_call_target="tpu_custom_call" | custom-call | tf_op jit(solution)/shard_map/pallas_call | solution.py:520
  55.6 1.4 %copy.3 = f32[256,32]{0,1:T(8,128)} copy(f32[256,32]{0,1:T(8,128)} %bitcast.1) | data formatting | bytes 65536

commit v6 on v5

--- a/solution.py
+++ b/solution.py
@@ -19,7 +19,7 @@
 SCALE = 2.0 / TOKENS
 PLANE = NX * NY * NC
 GATES = 1
-
+FIRST = 12
 
 def wait(ref, sem):
     pltpu.make_async_copy(ref, ref, sem).wait()
@@ -100,9 +100,9 @@
 
 
 def exchange(a_ref, out_ref, feats, slices, partial, inbox, total, pin, psum, tall, rows, cols, pivot, owned,
-             tz, ty, tq, tr, square, hubs, strip, many, gram, gin, gpart, gx, gtot,
+             tz, ty, tq, tr, square, hubs, strip, many, gram, gin, gpart, gx, gtot, block_in,
              g1_s, g1_r, sib_s, sib_r, sl_s, sl_r, z_s, z_r, tz_s, tz_r, ty_s, ty_r, p0_s, p0_r, p1_s, p1_r,
-             rows_s, rows_r, cols_s, cols_r, piv_s, piv_r, own_s, own_r, move_s, move_r, hub_s, hub_r, gz_s, gz_r, gx_s, gx_r, gate):
+             rows_s, rows_r, cols_s, cols_r, piv_s, piv_r, own_s, own_r, move_s, move_r, hub_s, hub_r, gz_s, gz_r, gx_s, gx_r, gate, in_sem):
     x, z, y, c = (lax.axis_index(name) for name in ("x", "z", "y", "c"))
     other = 1 - c
 
@@ -113,6 +113,8 @@
         return (lax.rem(x + i // (NY * NC), NX), z, lax.rem(y + i // NC, NY), lax.rem(c + i, NC))
 
     barrier = pltpu.get_barrier_semaphore()
+
+    local(a_ref, block_in, in_sem)
 
     @pl.loop(1, PLANE)
     def _(i):
@@ -122,11 +124,12 @@
     def _(d):
         pl.semaphore_signal(barrier, inc=1, device_id=along(d), device_id_type=MESH)
 
-    feats[c, x] = a_ref[...].T
+    wait(block_in, in_sem)
+    feats[c, x] = block_in[...].T
     pl.semaphore_wait(barrier, PLANE - 1 + NZ - 1)
     hub = both(y == 0, c == 0)
     panel = c == 0
-    place = lax.rem(z + 4, NZ)
+    place = lax.rem(z + NZ - FIRST, NZ)
     holder = both(panel, place < STRIPS)
     place_s, place_h = place // NC, lax.rem(place, NC)
 
@@ -162,7 +165,7 @@
         block = lax.dot_general(block, block, (((1,), (1,)), ((), ())), preferred_element_type=F32)
         gram[...] = block.reshape(STRIPS, 16, PANEL)
         for n in range(STRIPS):
-            target = (12 + n) % NZ
+            target = (FIRST + n) % NZ
             pl.when(target == z)(lambda: local(gram.at[n], gin.at[z], gz_r))
             pl.when(target != z)(lambda: send(gram.at[n], gin.at[z], gz_s, gz_r, (x, target, y, c)))
 
@@ -291,7 +294,7 @@
     @pl.when(panel)
     def _():
         for n in range(STRIPS):
-            target = (12 + n) % NZ
+            target = (FIRST + n) % NZ
 
             @pl.when(target == z)
             def _():
@@ -306,9 +309,8 @@
         wait(gx, gx_r)
         gtot[...] = jnp.sum(gx[...], axis=0)
 
-        @pl.loop(0, NZ - 1)
-        def _(d):
-            send(gtot, hubs.at[place], hub_s, hub_r, along(far_first(d)))
+        for d in (8, 7, 9, 6, 10, 5, 11, 4, 12, 3, 13, 2, 14, 1, 15):
+            send(gtot, hubs.at[place], hub_s, hub_r, along(d))
         local(gtot, hubs.at[place], hub_r)
 
     tracer = both(x == NX - 1, c == 1)
@@ -348,9 +350,8 @@
         wait(pin, p0_r)
         psum[...] = jnp.sum(pin[...], axis=0)
 
-        @pl.loop(0, NZ - 1)
-        def _(d):
-            send(psum, tall.at[place_h, place_s], p1_s, p1_r, along(far_first(d)))
+        for d in (8, 7, 9, 6, 10, 5, 11, 4, 12, 3, 13, 2, 14, 1, 15):
+            send(psum, tall.at[place_h, place_s], p1_s, p1_r, along(d))
         local(psum, tall.at[place_h, place_s], p1_r)
 
     pl.when(panel)(lambda: reduce_to_peers((2, 3), kept))
@@ -385,8 +386,7 @@
         local(hubs, pivot, piv_r)
 
     def spread(src, dst, sems, recv, count, where, start):
-        @pl.loop(0, count)
-        def _(i):
+        for i in range(count):
             tx, to_y, tc = where(i)
             here = both(tx == x, to_y == y, tc == c)
             if start:
@@ -396,9 +396,9 @@
                 pl.when(neither(here))(lambda: wait(src, sems.at[i]))
 
     def spread_panel(start):
+        spread(strip, cols.at[x], cols_s, cols_r, NY * NC, lambda i: (y, i // 2, lax.rem(i, NC)), start)
         for half in range(NC):
             spread(tall.at[half], rows.at[x], rows_s.at[half], rows_r, NX, lambda i: (lax.rem(x + i, NX), y, half), start)
-        spread(strip, cols.at[x], cols_s, cols_r, NY * NC, lambda i: (y, i // 2, lax.rem(i, NC)), start)
 
     @pl.when(panel)
     def _():
@@ -436,21 +436,21 @@
         diag = jnp.sum(jnp.where(lane == sub + 8 * g, groups[g][0], 0.0), axis=1, keepdims=True)
         scaled.append(groups[g][1] * lax.rsqrt(diag))
     inverse = jnp.concatenate(scaled, axis=0)
+    highest = lax.Precision.HIGHEST
     wait(cols, cols_r)
+    left = jnp.concatenate([pltpu.roll(cols[i], (128 - 32 * q) % 128, 1) for q in range(4) for i in range(NX)], axis=0)
+    left = jnp.dot(inverse, left * SCALE, precision=highest, preferred_element_type=F32)[:, :32]
     wait(rows, rows_r)
     ids = lax.broadcasted_iota(jnp.int32, (PANEL, BLOCK), 0)
     row0 = (y * NC + c) * BLOCK
     row_ids = row0 + lax.broadcasted_iota(jnp.int32, (PANEL, BLOCK), 1)
     right = jnp.concatenate([rows[i, q] for q in range(4) for i in range(NX)], axis=0)
     right = right * SCALE + jnp.where(ids == row_ids, damp, 0.0)
-    highest = lax.Precision.HIGHEST
     right = jnp.dot(inverse, right, precision=highest, preferred_element_type=F32)
-    left = jnp.concatenate([pltpu.roll(cols[i], (128 - 32 * q) % 128, 1) for q in range(4) for i in range(NX)], axis=0)
-    left = jnp.dot(inverse, left * SCALE, precision=highest, preferred_element_type=F32)
     update = lax.dot_general(left, right, (((0,), (0,)), ((), ())), precision=highest, preferred_element_type=F32)
     strip0 = (x * NZ + z) * 32
     leading = strip0 < PANEL
-    wide = update[:32]
+    wide = update
     for q in range(4):
         wide = jnp.where(both(leading, z == q), right[32 * q:32 * q + 32], wide)
     col_ids = strip0 + lax.broadcasted_iota(jnp.int32, (32, BLOCK), 0)
@@ -520,7 +520,7 @@
     result = pl.pallas_call(
         exchange,
         out_shape=jax.ShapeDtypeStruct((32, BLOCK), F32),
-        in_specs=[vmem],
+        in_specs=[pl.BlockSpec(memory_space=pl.ANY)],
         out_specs=vmem,
         scratch_shapes=[
             pltpu.VMEM((NC, NX, BLOCK, BLOCK), BF16),
@@ -548,6 +548,7 @@
             pltpu.VMEM((16, 128), F32),
             pltpu.VMEM((NX, 16, 128), F32),
             pltpu.VMEM((16, 128), F32),
+            pltpu.VMEM((BLOCK, BLOCK), BF16),
             dma((6,)), dma((NX, 2)),
             dma((NX,)), dma((NX,)),
             dma((NY, NX)), dma((NY, NX)),
@@ -564,7 +565,8 @@
             dma(()), dma(()),
             dma(()), dma(()),
             dma((NX,)), dma(()),
-            pltpu.SemaphoreType.REGULAR((2,)),
+            pltpu.SemaphoreType.REGULAR((1,)),
+            dma(()),
         ],
         compiler_params=pltpu.CompilerParams(collective_id=0, has_side_effects=True),
     )(a)

time: 57.1 us -> 56.4 us (0.988)
  Pallas kernels: 55.6 us -> 54.8 us
    pallas_call x1, Pallas kernels: 55.6 us -> 54.8 us  [shards(): pl.pallas_call(exchange, out_shape=jax.ShapeDtypeStruct((32, BLOCK), F32)...]
where the time goes in v6:
time: 56.4 us; the launch traced here: 56.2 us
  Pallas kernels  54.8 us (97%)
  local copies, waits for them, and re-layouts  1.38 us (2%)
    pallas_call x1, Pallas kernels, shards(): pl.pallas_call(exchange, out_shape=jax.ShapeDtypeStruct((32, BLOCK), F32)...  54.8 us
    unnamed x1, local copies, waits for them, and re-layouts  1.38 us

profile of v6, /device:TPU:120, one launch (start us, length us, event | category | flops | bytes accessed | tf_op | source)
XLA Modules:
  0.0 56.2 jit_solution(15654938110288367638)
XLA Ops:
  0.0 54.8 %shard_map.17 = f32[32,256]{1,0:T(8,128)} custom-call(bf16[256,256]{1,0:T(8,128)(2,1)} %a_ref.1), custom_call_target="tpu_custom_call" | custom-call | tf_op jit(solution)/shard_map/pallas_call | solution.py:520
  54.8 1.4 %copy.3 = f32[256,32]{0,1:T(8,128)} copy(f32[256,32]{0,1:T(8,128)} %bitcast.1) | data formatting | bytes 65536

commit v7 on v6

--- a/solution.py
+++ b/solution.py
@@ -361,7 +361,8 @@
         for n in range(GATES):
             pl.semaphore_signal(gate.at[n], inc=1, device_id=along(8), device_id_type=MESH)
             pl.semaphore_wait(gate.at[n], 1)
-        reduce_to_peers((0, 1, 2, 3), kept)
+        for k in range(NY):
+            reduce_to_peers((k,), kept)
 
     taken_in(2)
     pl.when(taken[2])(lambda: reduce_to_peers((2,), active))

time: 56.4 us -> 56.4 us (level)
  no operation moved by 1% of the time
where the time goes in v7:
time: 56.4 us; the launch traced here: 56.2 us
  Pallas kernels  54.8 us (97%)
  local copies, waits for them, and re-layouts  1.38 us (2%)
    pallas_call x1, Pallas kernels, shards(): pl.pallas_call(exchange, out_shape=jax.ShapeDtypeStruct((32, BLOCK), F32)...  54.8 us
    unnamed x1, local copies, waits for them, and re-layouts  1.38 us

profile of v7, /device:TPU:120, one launch (start us, length us, event | category | flops | bytes accessed | tf_op | source)
XLA Modules:
  0.0 56.2 jit_solution(4579336409748904727)
XLA Ops:
  0.0 54.8 %shard_map.17 = f32[32,256]{1,0:T(8,128)} custom-call(bf16[256,256]{1,0:T(8,128)(2,1)} %a_ref.1), custom_call_target="tpu_custom_call" | custom-call | tf_op jit(solution)/shard_map/pallas_call | solution.py:521
  54.8 1.4 %copy.3 = f32[256,32]{0,1:T(8,128)} copy(f32[256,32]{0,1:T(8,128)} %bitcast.1) | data formatting | bytes 65536

commit v8 on v7

--- a/solution.py
+++ b/solution.py
@@ -343,7 +343,7 @@
     def kept(k):
         return both(active(k), neither(taken[k])) if k in taken else active(k)
 
-    pl.when(panel)(lambda: reduce_to_peers((0, 1), kept))
+    pl.when(panel)(lambda: [reduce_to_peers((k,), kept) for k in (1, 0)] and None)
 
     @pl.when(holder)
     def _():

time: 56.4 us -> 56.3 us (level)
  the two profiles are of different devices: /device:TPU:120 before, /device:TPU:26 now
where the time goes in v8:
time: 56.3 us; the launch traced here: 56.1 us
  Pallas kernels  54.7 us (97%)
  local copies, waits for them, and re-layouts  1.38 us (2%)
    pallas_call x1, Pallas kernels, shards(): pl.pallas_call(exchange, out_shape=jax.ShapeDtypeStruct((32, BLOCK), F32)...  54.7 us
    unnamed x1, local copies, waits for them, and re-layouts  1.38 us

profile of v8, /device:TPU:26, one launch (start us, length us, event | category | flops | bytes accessed | tf_op | source)
XLA Modules:
  0.0 56.1 jit_solution(10756491837958477477)
XLA Ops:
  0.0 54.7 %shard_map.17 = f32[32,256]{1,0:T(8,128)} custom-call(bf16[256,256]{1,0:T(8,128)(2,1)} %a_ref.1), custom_call_target="tpu_custom_call" | custom-call | tf_op jit(solution)/shard_map/pallas_call | solution.py:521
  54.7 1.4 %copy.3 = f32[256,32]{0,1:T(8,128)} copy(f32[256,32]{0,1:T(8,128)} %bitcast.1) | data formatting | bytes 65536
